TPU v7x, 32 devices: a whole 2x2x4 slice. The times are simulated.
32 devices in a mesh: slab: 32 (over z, y, x, core).
Axes of the slice: x: 2, y: 2, z: 4, core: 2. Of those that a mesh axis runs over, the one named last changes fastest.
Arguments:
- start_vectors: float32 [2, 32, 256, 256], P(None, 'slab'), may hold values from -6 to 6
- levels: int32 [32, 256, 256], P('slab'), may hold values from 0 to 15
- energies: float32 [16], replicated, may hold values from -4 to 4
Outputs:
- cheb_field: float32 [2, 32, 256, 256], P(None, 'slab')
- lanczos_diag: float32 [2, 8], replicated
- lanczos_off: float32 [2, 7], replicated
- moments: float32 [2, 6], replicated
All inputs are finite; a program needn't handle non-finite values.
Results may differ from a plain program's by a relative error of at most 0.0001.
Values sent between devices are 32-bit elements; how exact they have to be, the bound alone decides.
A program may use at most 64 MiB of HBM per device.

v0:
```python
import functools

import jax
import jax.numpy as jnp
from jax import lax
from jax.experimental import pallas as pl
from jax.experimental.pallas import tpu as pltpu
from jax.sharding import PartitionSpec as P

LANCZOS = 8
HALF = LANCZOS // 2
GROUP = 8
GHOST = 8
RETURNED = 3


def phase_one(dots, half, sqrt):
    norm = dots[0]
    nu = [None] * len(dots)
    nu[0] = norm / norm
    nu[1] = dots[1] / norm
    for k in range(2, len(dots)):
        nu[k] = 2.0 * dots[k] / norm - nu[k % 2]
    top = len(nu) - 1
    row, before = list(nu), None
    diag, offd = [], []
    for k in range(half):
        if k == 0:
            alpha = row[1]
        else:
            alpha = (0.5 * row[k + 1] - offd[-1] * before[k]) / row[k]
        diag.append(alpha)
        new = [None] * len(nu)
        for l in range(k + 1, top - k):
            new[l] = 0.5 * (row[l + 1] + row[l - 1]) - alpha * row[l]
            if k:
                new[l] = new[l] - offd[-1] * before[l]
        beta = sqrt(new[k + 1] / (row[k] if k == 0 else 2.0 * row[k]))
        offd.append(beta)
        inv = 1.0 / beta
        before, row = row, [None if x is None else x * inv for x in new]
    zero = nu[0] * 0.0
    scale = 1.0 / sqrt(norm)
    vectors = [[scale] + [zero] * half]
    for k in range(half):
        now = vectors[-1]
        inv = 1.0 / offd[k]
        shifted = [zero] * (half + 1)
        for l in range(k + 1):
            if l == 0:
                shifted[1] = shifted[1] + now[0]
            else:
                shifted[l + 1] = shifted[l + 1] + 0.5 * now[l]
                shifted[l - 1] = shifted[l - 1] + 0.5 * now[l]
        new = [shifted[l] - diag[k] * now[l] for l in range(half + 1)]
        if k:
            new = [x - offd[k - 1] * y for x, y in zip(new, vectors[-2])]
        vectors.append([x * inv for x in new])
    return nu, diag, offd, vectors


def phase_two(dots, diag, offd, half, sqrt):
    count = len(dots)
    gram = {}
    for k, value in enumerate(dots):
        gram[(half + k // 2, half + (k + 1) // 2)] = value
    zero = dots[0] * 0.0
    one = zero + 1.0
    for k in range(half):
        gram[(k, half)] = zero
        gram[(k, half - 1)] = one if k == half - 1 else zero
    guess_a, guess_b = diag[half - 1], offd[half - 1]
    inv = 1.0 / guess_b

    def entry(i, j):
        if (i, j) in gram:
            return gram[(i, j)]
        if j > half and i < half and (j - half) < (half - i) + 1:
            value = zero
        elif i >= half:
            value = entry(i + 1, j - 1) + entry(i - 1, j - 1) - entry(i, j - 2)
        else:
            value = (offd[i] * inv) * entry(i + 1, j - 1) - entry(i, j - 2)
            if i != half - 1:
                value = value + ((diag[i] - guess_a) * inv) * entry(i, j - 1)
            if i > 0:
                value = value + (offd[i - 1] * inv) * entry(i - 1, j - 1)
        gram[(i, j)] = value
        return value

    top = half + count - 1
    row = {l: entry(half, l) for l in range(half, top + 1)}
    before = {l: entry(half - 1, l) for l in range(half, top)}
    diag, offd = list(diag), list(offd)
    for k in range(half, 2 * half):
        if k == half:
            alpha = guess_a + guess_b * row[k + 1] / row[k]
        else:
            alpha = guess_a + (guess_b * row[k + 1] - offd[k - 1] * before[k]) / row[k]
        diag.append(alpha)
        if k == 2 * half - 1:
            break
        new = {}
        for l in range(k + 1, top - (k - half)):
            new[l] = guess_b * (row[l + 1] + row[l - 1]) + (guess_a - alpha) * row[l] - offd[k - 1] * before[l]
        beta = sqrt(new[k + 1] * guess_b / row[k])
        offd.append(beta)
        inv_b = 1.0 / beta
        before, row = row, {l: x * inv_b for l, x in new.items()}
    return diag, offd


def chebyshev(diag, offd, nu, centre, width):
    left = [None] + offd
    right = offd + [None]
    low, high = None, None
    for a, b, c in zip(diag, left, right):
        reach = b if c is None else c if b is None else b + c
        low = a - reach if low is None else jnp.minimum(low, a - reach)
        high = a + reach if high is None else jnp.maximum(high, a + reach)
    inv = 1.0 / (0.55 * (high - low))
    al = width * inv
    be = (centre - 0.5 * (high + low)) * inv
    p, q, r = 2.0 * be * be + al * al - 1.0, 4.0 * al * be, al * al
    first = [be, al]
    second = [p, q, r]
    third = [2.0 * be * p + al * q - be, 2.0 * be * q + al * (2.0 * p + r) - al, 2.0 * be * r + al * q, al * r]

    def dot(f, g):
        total = None
        for i, x in enumerate(f):
            for j, y in enumerate(g):
                term = (x * y) * (0.5 * (nu[i + j] + nu[abs(i - j)]))
                total = term if total is None else total + term
        return total

    start = [nu[0]]
    m1 = dot(start, first)
    moments = [
        m1,
        dot(start, second),
        dot(start, third),
        2.0 * dot(second, second) - 1.0,
        2.0 * dot(third, second) - m1,
        2.0 * dot(third, third) - 1.0,
    ]
    return third, moments


def kernel(
    count, energies, start, levels, cheb, diag_out, offd_out, moments_out,
    own, own_levels, field, halo, onsite, level, back, part, part_far, mine,
    load_sem, vec_sem, level_sem, halo_send, halo_recv, back_send, back_recv, red_send, red_recv,
):
    me = lax.axis_index("slab")
    member = lax.rem(me, GROUP)
    group = me // GROUP
    base = me - member
    groups = count // GROUP
    vecs, _, height, lanes = start.shape
    my_vec, block = lax.rem(member, vecs), member // vecs
    rows = height // (GROUP // vecs)
    deep = rows + 2 * GHOST
    mesh_id = pl.DeviceIdType.MESH
    ahead = lax.rem(me + GROUP, count)
    behind = lax.rem(me + count - GROUP, count)

    loads = [
        pltpu.make_async_copy(start.at[:, 0], own, load_sem.at[0]),
        pltpu.make_async_copy(levels.at[0], own_levels, load_sem.at[1]),
    ]
    for copy in loads:
        copy.start()

    def peer(i):
        return base + lax.rem(member + i, GROUP)

    def far(i):
        return lax.rem(me + i * GROUP, count)

    barrier = pltpu.get_barrier_semaphore()

    def greet(i, carry):
        pl.semaphore_signal(barrier, inc=1, device_id=(peer(i),), device_id_type=mesh_id)
        return carry

    def greet_far(i, carry):
        pl.semaphore_signal(barrier, inc=1, device_id=(far(i),), device_id_type=mesh_id)
        return carry

    lax.fori_loop(1, GROUP, greet, 0)
    lax.fori_loop(1, groups, greet_far, 0)
    pl.semaphore_wait(barrier, GROUP - 1 + groups - 1)

    def pieces(i):
        i = i // vecs
        mid = pl.multiple_of(i * rows, 8)
        top = pl.multiple_of(lax.rem(i * rows + height - GHOST, height), 8)
        low = pl.multiple_of(lax.rem(i * rows + rows, height), 8)
        return ((mid, GHOST, rows), (top, 0, GHOST), (low, GHOST + rows, GHOST))

    def vec_refs(i):
        return [
            (own.at[lax.rem(i, vecs), pl.ds(at, size)], field.at[0, member, pl.ds(to, size)])
            for at, to, size in pieces(i)
        ]

    def level_refs(i):
        return [
            (own_levels.at[pl.ds(at, size)], level.at[member, pl.ds(to, size)])
            for at, to, size in pieces(i)
        ]

    def scatter(refs, sems):
        def body(i, carry):
            to = lax.rem(member + i, GROUP)
            for src, dst in refs(to):
                pltpu.make_async_remote_copy(
                    src_ref=src, dst_ref=dst, send_sem=sems.at[0], recv_sem=sems.at[1],
                    device_id=(base + to,), device_id_type=mesh_id,
                ).start()
            return carry

        lax.fori_loop(1, GROUP, body, 0)
        for src, dst in refs(member):
            pltpu.make_async_copy(src, dst, sems.at[1]).start()

    def drain(ref, sem):
        pltpu.make_async_copy(ref, ref, sem).wait()

    loads[0].wait()
    scatter(vec_refs, vec_sem)
    loads[1].wait()
    scatter(level_refs, level_sem)

    values = [energies[i] for i in range(energies.shape[0])]
    mean = sum(values[1:], values[0]) * (1.0 / len(values))
    spread = [(x - mean) * (x - mean) for x in values]
    spread = sum(spread[1:], spread[0]) * (1.0 / len(values))
    width = 2.0 * jnp.sqrt(jnp.full((1, lanes), spread + 6.0, jnp.float32))
    inv_width = 1.0 / width

    def halo_copies(slot, at):
        part_of = pl.ds(GHOST, rows) if at == LANCZOS - 1 else pl.ds(0, deep)
        return [
            pltpu.make_async_remote_copy(
                src_ref=field.at[slot, plane, part_of], dst_ref=halo.at[at, side, part_of],
                send_sem=halo_send.at[at, side], recv_sem=halo_recv.at[at, side],
                device_id=(to,), device_id_type=mesh_id,
            )
            for plane, side, to in ((0, 1, behind), (GROUP - 1, 0, ahead))
        ]

    def give_back(k):
        def refs(i):
            return (
                field.at[k, i, pl.ds(GHOST, rows)],
                back.at[k - 1, my_vec, pl.ds(pl.multiple_of(block * rows, 8), rows)],
            )

        def body(i, carry):
            to = lax.rem(member + i, GROUP)
            src, dst = refs(to)
            pltpu.make_async_remote_copy(
                src_ref=src, dst_ref=dst, send_sem=back_send.at[k - 1], recv_sem=back_recv.at[k - 1],
                device_id=(base + to,), device_id_type=mesh_id,
            ).start()
            return carry

        lax.fori_loop(1, GROUP, body, 0)
        src, dst = refs(member)
        pltpu.make_async_copy(src, dst, back_recv.at[k - 1]).start()

    def tile_sum(x):
        x = x[GHOST : GHOST + rows]
        total = x[0:8]
        for i in range(8, rows, 8):
            total = total + x[i : i + 8]
        return total

    def step(source, target, before, at, combine, awaited, extra=False):
        nothing = jnp.zeros((8, lanes), jnp.float32)

        def local(m, here, *beside):
            near = pltpu.roll(here, 1, 0) + pltpu.roll(here, deep - 1, 0)
            near = near + pltpu.roll(here, 1, 1) + pltpu.roll(here, lanes - 1, 1)
            for plane in beside:
                near = near + field[source, plane]
            return onsite[m] * here - inv_width * near

        def finish(m, here, applied):
            new = combine(applied, here, None if before is None else field[before, m])
            if target is not None:
                field[target, m] = new
            return new

        def add(sums, here, new):
            sums = list(sums)
            sums[0] = sums[0] + tile_sum(here * new)
            sums[1] = sums[1] + tile_sum(new * new)
            if extra:
                sums[2] = sums[2] + tile_sum(here * here)
            return tuple(sums)

        def plane(m, sums):
            here = field[source, m]
            return add(sums, here, finish(m, here, local(m, here, m - 1, m + 1)))

        faces = ((0, 1), (GROUP - 1, GROUP - 2))
        parts = [local(m, field[source, m], inner) for m, inner in faces]
        for copy in awaited:
            copy.wait_recv()
        news = [
            finish(m, field[source, m], part - inv_width * halo[at, side])
            for side, ((m, inner), part) in enumerate(zip(faces, parts))
        ]
        sent = []
        if target is not None:
            sent = halo_copies(target, at + 1)
            for copy in sent:
                copy.start()
        sums = (nothing,) * 3
        for (m, inner), new in zip(faces, news):
            sums = add(sums, field[source, m], new)
        sums = lax.fori_loop(
            1,
            GROUP - 1,
            plane,
            sums,
            unroll=3,
        )
        return sums, sent

    lane = lax.broadcasted_iota(jnp.int32, (8, 128), 1)
    line = lax.broadcasted_iota(jnp.int32, (8, 128), 0)

    def reduce_all(dots, turn):
        tile = jnp.zeros((8, 128), jnp.float32)
        for d, value in enumerate(dots):
            whole = jnp.sum(jnp.sum(value, axis=0, keepdims=True), axis=1, keepdims=True)
            tile = jnp.where((lane == d) & (line == my_vec), whole, tile)
        for leg, (slots, index, size, target) in enumerate(
            ((part.at[turn], member, GROUP, peer), (part_far.at[turn], group, groups, far))
        ):
            mine[turn, leg] = tile
            slots[index] = tile

            def body(i, carry):
                pltpu.make_async_remote_copy(
                    src_ref=mine.at[turn, leg], dst_ref=slots.at[index],
                    send_sem=red_send.at[turn, leg], recv_sem=red_recv.at[turn, leg],
                    device_id=(target(i),), device_id_type=mesh_id,
                ).start()
                return carry

            lax.fori_loop(1, size, body, 0)
            drain(slots.at[pl.ds(0, size - 1)], red_recv.at[turn, leg])
            tile = slots[0]
            for i in range(1, size):
                tile = tile + slots[i]
        return [
            jnp.broadcast_to(tile[0:vecs, d : d + 1], (vecs, lanes)) for d in range(len(dots))
        ]

    drain(field.at[0], vec_sem.at[1])
    sent = [halo_copies(0, 0)]
    for copy in sent[0]:
        copy.start()
    drain(level, level_sem.at[1])

    def look_up(m, carry):
        ids = level[m]
        energy = jnp.full(ids.shape, values[0] - mean, jnp.float32)
        for i in range(1, len(values)):
            energy = jnp.where(ids == i, values[i] - mean, energy)
        onsite[m] = energy * inv_width
        return carry

    lax.fori_loop(0, GROUP, look_up, 0)

    def arrive(copies):
        for copy in copies:
            copy.wait_recv()

    dots = [None]
    for k in range(HALF):
        if k == 0:
            rule = lambda applied, here, old: applied
        else:
            rule = lambda applied, here, old: 2.0 * applied - old
        sums, copies = step(k, k + 1, k - 1 if k else None, k, rule, sent[k], extra=k == 0)
        sent.append(copies)
        if k == 0:
            dots[0] = sums[2]
        dots.append(sums[0])
        dots.append(sums[1])
        if k + 1 <= RETURNED:
            give_back(k + 1)

    totals = reduce_all(dots, 0)
    nu, diag, offd, vectors = phase_one(totals, HALF, jnp.sqrt)
    arrive(sent[HALF])
    old_at, new_at = HALF + 1, HALF + 2

    def mix(coefficients, read):
        total = coefficients[0] * read(0)
        for k in range(1, len(coefficients)):
            total = total + coefficients[k] * read(k)
        return total

    which = jnp.full((1, lanes), my_vec, jnp.int32)

    def pick(value):
        row = value[0:1]
        for v in range(1, vecs):
            row = jnp.where(which == v, value[v : v + 1], row)
        return row

    old_mix = [pick(x) for x in vectors[HALF - 1][:HALF]]
    new_mix = [pick(x) for x in vectors[HALF]]
    for side in range(2):
        halo[HALF, side] = mix(new_mix, lambda k: halo[k, side])

    def restart(m, total):
        field[old_at, m] = mix(old_mix, lambda k: field[k, m])
        new = mix(new_mix, lambda k: field[k, m])
        field[new_at, m] = new
        return total + tile_sum(new * new)

    dots = [
        lax.fori_loop(0, GROUP, restart, jnp.zeros((8, lanes), jnp.float32), unroll=2)
    ]
    gain = pick(1.0 / offd[HALF - 1])
    shift = pick(diag[HALF - 1])

    def rule(applied, here, old):
        return gain * (applied - shift * here) - old

    for k in range(HALF):
        at = HALF + k
        last = k == HALF - 1
        sums, copies = step(new_at + k, None if last else new_at + k + 1, new_at + k - 1, at, rule, sent[at] if k else [])
        sent.append(copies)
        dots.append(sums[0])
        if not last:
            dots.append(sums[1])

    totals = reduce_all(dots, 1)
    diag, offd = phase_two(totals, diag, offd, HALF, jnp.sqrt)
    diag = [width * a + mean for a in diag]
    offd = [width * b for b in offd]
    third, moments = chebyshev(diag, offd, nu, mean, width)

    for k in range(RETURNED):
        drain(back.at[k], back_recv.at[k])
    for v in range(vecs):
        cheb[v, 0] = mix([x[v : v + 1] for x in third], lambda k: own[v] if k == 0 else back[k - 1, v])

    for ref, items in ((diag_out, diag), (offd_out, offd), (moments_out, moments)):
        at = lax.broadcasted_iota(jnp.int32, ref.shape, 1)
        value = jnp.zeros(ref.shape, jnp.float32)
        for i, item in enumerate(items):
            value = jnp.where(at == i, item[:, : ref.shape[1]], value)
        ref[...] = value

    for copies in sent:
        for copy in copies:
            copy.wait_send()
    drain(field.at[0, pl.ds(0, GROUP - 1)], vec_sem.at[0])
    drain(level.at[pl.ds(0, GROUP - 1)], level_sem.at[0])
    for k in range(RETURNED):
        drain(field.at[k + 1, pl.ds(0, GROUP - 1), pl.ds(GHOST, rows)], back_send.at[k])
    for turn in range(2):
        drain(part.at[turn, pl.ds(0, GROUP - 1)], red_send.at[turn, 0])
        drain(part_far.at[turn, pl.ds(0, groups - 1)], red_send.at[turn, 1])


def shards(count, start_vectors, levels, energies):
    vecs, _, height, lanes = start_vectors.shape
    groups = count // GROUP
    deep = height // (GROUP // vecs) + 2 * GHOST
    f32 = jnp.float32
    vmem = pl.BlockSpec(memory_space=pltpu.VMEM)
    anywhere = pl.BlockSpec(memory_space=pl.ANY)
    dma = pltpu.SemaphoreType.DMA
    return pl.pallas_call(
        functools.partial(kernel, count),
        out_shape=(
            jax.ShapeDtypeStruct(start_vectors.shape, f32),
            jax.ShapeDtypeStruct((vecs, LANCZOS), f32),
            jax.ShapeDtypeStruct((vecs, LANCZOS - 1), f32),
            jax.ShapeDtypeStruct((vecs, 6), f32),
        ),
        in_specs=[pl.BlockSpec(memory_space=pltpu.SMEM), anywhere, anywhere],
        out_specs=(vmem,) * 4,
        scratch_shapes=[
            pltpu.VMEM((vecs, height, lanes), f32),
            pltpu.VMEM((height, lanes), jnp.int32),
            pltpu.VMEM((LANCZOS + 2, GROUP, deep, lanes), f32),
            pltpu.VMEM((LANCZOS, 2, deep, lanes), f32),
            pltpu.VMEM((GROUP, deep, lanes), f32),
            pltpu.VMEM((GROUP, deep, lanes), jnp.int32),
            pltpu.VMEM((RETURNED, vecs, height, lanes), f32),
            pltpu.VMEM((2, GROUP, 8, 128), f32),
            pltpu.VMEM((2, groups, 8, 128), f32),
            pltpu.VMEM((2, 2, 8, 128), f32),
            dma((2,)),
            dma((2,)),
            dma((2,)),
            dma((LANCZOS, 2)),
            dma((LANCZOS, 2)),
            dma((RETURNED,)),
            dma((RETURNED,)),
            dma((2, 2)),
            dma((2, 2)),
        ],
        compiler_params=pltpu.CompilerParams(
            collective_id=0, has_side_effects=True, vmem_limit_bytes=67043328
        ),
    )(energies, start_vectors, levels)


def solution(mesh):
    in_specs = (P(None, "slab", None, None), P("slab", None, None), P())
    out_specs = (P(None, "slab", None, None), P(), P(), P())
    return jax.shard_map(
        functools.partial(shards, mesh.shape["slab"]),
        mesh=mesh, in_specs=in_specs, out_specs=out_specs, check_vma=False,
    )
```

profile of v0, /device:TPU:0, one launch (start us, length us, event | category | flops | bytes accessed | tf_op | source)
XLA Modules:
  0.0 74.6 jit_solution(9182451934973270311)
XLA Ops:
  0.6 70.1 %shard_map.66 = (f32[2,1,256,256]{3,2,1,0:T(8,128)}, f32[2,8]{1,0:T(2,128)}, f32[2,7]{1,0:T(2,128)}, f32[2,6]{1,0:T(2,128)}) custom-call(f32[16]{0:T(128)} %energies.1, f32[2,1,256,256]{3,2,1,0:T(8,128)} %start.1, s32[1,256,256]{2,1,0:T(8,128)} %levels.1), custom_call_target="tpu_custom_call" | custom-call | tf_op jit(solution)/shard_map/pallas_call | solution.py:486
  70.8 0.0 copy-start.2
  70.8 1.9 %copy.11 = f32[2,1,256,256]{3,2,1,0:T(8,128)} copy(f32[2,1,256,256]{3,2,1,0:T(8,128)} %get-tuple-element.8) | data formatting | bytes 1048576
  72.7 0.0 copy-done.2
  72.7 0.0 copy-start.1
  72.7 0.6 copy.12
  73.2 0.1 copy-done.1
  73.3 0.0 copy-start
  73.3 0.6 copy.13
  73.9 0.1 copy-done
  74.0 0.6 copy.14
Async XLA Ops:
  70.8 1.9 %copy-start.2 = (f32[2,8]{1,0:T(2,128)S(1)}, f32[2,8]{1,0:T(2,128)}, u32[]{:S(2)}) copy-start(f32[2,8]{1,0:T(2,128)} %get-tuple-element.9) | copy-start | bytes 196
  72.7 0.7 copy-start.1
  73.3 0.7 copy-start
where the time goes:
time: 74.7 us; the launch traced here: 74.6 us
  Pallas kernels  70.1 us (94%)
  local copies, waits for them, and re-layouts  3.76 us (5%)
    pallas_call x1, Pallas kernels, shards(): pl.pallas_call(functools.partial(kernel, count), out_shape=(jax.ShapeDtyp...  70.1 us
    unnamed x10, local copies, waits for them, and re-layouts  3.76 us

commit v1 on v0

v1 whole, which is shorter than its diff:
```python
import functools

import jax
import jax.numpy as jnp
from jax import lax
from jax.experimental import pallas as pl
from jax.experimental.pallas import tpu as pltpu
from jax.sharding import PartitionSpec as P

LANCZOS = 8
ROUNDS = LANCZOS // 2
GROUP = 8
RETURNED = 3


def lanczos(dots, steps, sqrt):
    norm = dots[0]
    inv_norm = 1.0 / norm
    nu = [None] * len(dots)
    nu[0] = norm * 0.0 + 1.0
    nu[1] = dots[1] * inv_norm
    for k in range(2, len(dots)):
        nu[k] = 2.0 * (dots[k] * inv_norm) - nu[k % 2]
    top = len(nu) - 1
    row, before = list(nu), None
    diag, offd = [], []
    for k in range(steps):
        if k == 0:
            alpha = row[1]
        else:
            alpha = (0.5 * row[k + 1] - offd[-1] * before[k]) / row[k]
        diag.append(alpha)
        if k == steps - 1:
            break
        new = [None] * len(nu)
        for l in range(k + 1, top - k):
            new[l] = 0.5 * (row[l + 1] + row[l - 1]) - alpha * row[l]
            if k:
                new[l] = new[l] - offd[-1] * before[l]
        beta = sqrt(new[k + 1] / (row[k] if k == 0 else 2.0 * row[k]))
        offd.append(beta)
        inv = 1.0 / beta
        before, row = row, [None if x is None else x * inv for x in new]
    return nu, diag, offd


def chebyshev(diag, offd, nu, centre, width):
    left = [None] + offd
    right = offd + [None]
    low, high = None, None
    for a, b, c in zip(diag, left, right):
        reach = b if c is None else c if b is None else b + c
        low = a - reach if low is None else jnp.minimum(low, a - reach)
        high = a + reach if high is None else jnp.maximum(high, a + reach)
    inv = 1.0 / (0.55 * (high - low))
    al = width * inv
    be = (centre - 0.5 * (high + low)) * inv
    p, q, r = 2.0 * be * be + al * al - 1.0, 4.0 * al * be, al * al
    first = [be, al]
    second = [p, q, r]
    third = [2.0 * be * p + al * q - be, 2.0 * be * q + al * (2.0 * p + r) - al, 2.0 * be * r + al * q, al * r]

    def dot(f, g):
        total = None
        for i, x in enumerate(f):
            for j, y in enumerate(g):
                term = (x * y) * (0.5 * (nu[i + j] + nu[abs(i - j)]))
                total = term if total is None else total + term
        return total

    start = [nu[0]]
    m1 = dot(start, first)
    moments = [
        m1,
        dot(start, second),
        dot(start, third),
        2.0 * dot(second, second) - 1.0,
        2.0 * dot(third, second) - m1,
        2.0 * dot(third, third) - 1.0,
    ]
    return third, moments


def ring_place(chip):
    return chip + lax.rem(chip // 2, 2) * (1 - 2 * lax.rem(chip, 2))


def kernel(
    count, energies, start, levels, cheb, diag_out, offd_out, moments_out,
    own, own_levels, field, twice, level, back,
    plane_in, partial_in, partial_out, edge_in, edge_out, edge, corner_in, corner_out, slots, mine,
    load_sem, vec_sem, level_in, level_sem, plane_sem, partial_sem, edge_sem, corner_sem, back_sem, sum_sem,
):
    me = lax.axis_index("slab")
    member = lax.rem(me, GROUP)
    base = me - member
    vecs, _, height, lanes = start.shape
    blocks = GROUP // vecs
    rows = height // blocks
    core, chip = lax.rem(member, vecs), member // vecs
    block = ring_place(chip)
    mesh_id = pl.DeviceIdType.MESH
    ahead_base = lax.rem(base + GROUP, count)
    behind_base = lax.rem(base + count - GROUP, count)
    above = ring_place(lax.rem(block + blocks - 1, blocks)) * vecs + core
    below = ring_place(lax.rem(block + 1, blocks)) * vecs + core
    partner = base + chip * vecs + lax.rem(core + 1, vecs)
    last = GROUP - 1

    loads = [
        pltpu.make_async_copy(start.at[:, 0], own, load_sem.at[0]),
        pltpu.make_async_copy(levels.at[0], own_levels, load_sem.at[1]),
    ]
    for copy in loads:
        copy.start()

    def remote(src, dst, send, recv, to):
        return pltpu.make_async_remote_copy(
            src_ref=src, dst_ref=dst, send_sem=send, recv_sem=recv, device_id=(to,), device_id_type=mesh_id
        )

    def drain(ref, sem):
        pltpu.make_async_copy(ref, ref, sem).wait()

    barrier = pltpu.get_barrier_semaphore()

    def greet(to):
        pl.semaphore_signal(barrier, inc=1, device_id=(to,), device_id_type=mesh_id)

    def greet_member(i, carry):
        greet(base + lax.rem(member + i, GROUP))
        return carry

    for side in (behind_base, ahead_base):
        for place in (member, above, below):
            greet(side + place)
    lax.fori_loop(1, GROUP, greet_member, 0)
    pl.semaphore_wait(barrier, GROUP - 1 + 6)

    def rows_of(at):
        return pl.ds(pl.multiple_of(at * rows, 8), rows)

    loads[0].wait()

    def scatter_vec(i, carry):
        to = lax.rem(member + i, GROUP)
        src = own.at[lax.rem(to, vecs), rows_of(ring_place(to // vecs))]
        remote(src, field.at[0, member], vec_sem.at[0], vec_sem.at[1], base + to).start()
        return carry

    lax.fori_loop(1, GROUP, scatter_vec, 0)
    pltpu.make_async_copy(own.at[core, rows_of(block)], field.at[0, member], vec_sem.at[1]).start()
    loads[1].wait()

    def scatter_level(i, carry):
        to = lax.rem(chip + i, blocks)
        src = own_levels.at[rows_of(ring_place(to))]
        remote(src, level.at[member], level_sem.at[0], level_in.at[chip], base + to * vecs + core).start()
        return carry

    lax.fori_loop(1, blocks, scatter_level, 0)
    pltpu.make_async_copy(own_levels.at[rows_of(block)], level.at[member], level_in.at[chip]).start()

    values = [energies[i] for i in range(energies.shape[0])]
    share = 1.0 / len(values)

    def total(terms):
        return sum(terms[1:], terms[0])

    mean = total(values) * share
    apart = [x - mean for x in values]
    square = [x * x for x in apart]
    second = total(square) * share + 6.0
    cube = total([x * y for x, y in zip(square, apart)]) * share
    fourth = total([x * x for x in square]) * share + 24.0 * (second - 6.0) + 90.0
    inv_second = 1.0 / jnp.full((1, lanes), second, jnp.float32)
    skew = cube * inv_second
    centre = mean + 0.5 * skew
    width = jnp.sqrt(2.0 * (fourth * inv_second - skew * skew))
    scale = 2.0 / width

    sub = lax.broadcasted_iota(jnp.int32, (8, lanes), 0)
    zero_row = jnp.zeros((1, lanes), jnp.float32)

    def look_up(m):
        ids = level[m]
        found = [jnp.full(ids.shape, x, jnp.float32) for x in values]
        bit = 1
        while len(found) > 1:
            odd = (ids & bit) != 0
            found = [
                found[i] if i + 1 == len(found) else jnp.where(odd, found[i + 1], found[i])
                for i in range(0, len(found), 2)
            ]
            bit *= 2
        twice[m] = (found[0] - centre) * scale

    def z_copies(r, k):
        return [
            remote(
                field.at[k, m], plane_in.at[r, 1 - z],
                plane_sem.at[0, r, z], plane_sem.at[1, r, 1 - z], side + member,
            )
            for z, m, side in ((0, 0, behind_base), (1, last, ahead_base))
        ]

    def q_copies(r):
        sides = ((0, behind_base), (1, ahead_base))
        return [
            remote(
                partial_out.at[r, z], partial_in.at[r, 1 - z],
                partial_sem.at[0, r, z], partial_sem.at[1, r, 1 - z], side + member,
            )
            for z, side in (sides[:1] if r == ROUNDS - 1 else sides)
        ]

    def y_copies(r, kind):
        return [
            remote(
                edge_out.at[r, kind, y], edge_in.at[r, kind, 1 - y],
                edge_sem.at[0, r, kind], edge_sem.at[1, r, kind], base + place,
            )
            for y, place in ((0, above), (1, below))
        ]

    def corner_copies(r):
        return [
            remote(
                corner_out.at[r, 2 * z + y], corner_in.at[r, 2 * (1 - z) + (1 - y)],
                corner_sem.at[0, r], corner_sem.at[1, r], side + place,
            )
            for z, side in ((0, behind_base), (1, ahead_base))
            for y, place in ((0, above), (1, below))
        ]

    def begin(copies):
        for copy in copies:
            copy.start()

    def put_corners(r, z, value):
        corner_out[r, 2 * z] = value[0:1]
        corner_out[r, 2 * z + 1] = value[rows - 1 : rows]

    def put_edges(r, kind, m, value):
        edge_out[r, kind, 0, m] = value[0:1]
        edge_out[r, kind, 1, m] = value[rows - 1 : rows]

    def around(here, top, bottom):
        up, down = pltpu.roll(here, 1, 0), pltpu.roll(here, rows - 1, 0)
        first = jnp.where(sub == 0, top, up[0:8])
        final = jnp.where(sub == 7, bottom, down[rows - 8 :])
        near = jnp.concatenate([first, up[8:]], 0) + jnp.concatenate([down[: rows - 8], final], 0)
        return near + (pltpu.roll(here, 1, 1) + pltpu.roll(here, lanes - 1, 1))

    def partial(k, m, *beside):
        here = field[k, m]
        near = around(here, zero_row, zero_row)
        for plane in beside:
            near = near + field[k, plane]
        new = twice[m] * here - scale * near
        new = 0.5 * new if k == 0 else new - field[k - 1, m]
        field[k + 1, m] = new
        return new

    def tile_sum(x):
        parts = [x[i : i + 8] for i in range(0, rows, 8)]
        while len(parts) > 1:
            parts = [a + b for a, b in zip(parts[::2], parts[1::2])]
        return parts[0]

    def follow(k, m, near, sums):
        here, old = field[k + 1, m], field[k, m]
        near = near + around(here, edge[0, m], edge[1, m])
        new = twice[m] * here - scale * near - old
        terms = [old * here, here * here, here * new]
        if k + 2 < LANCZOS:
            field[k + 2, m] = new
            put_edges(k // 2 + 1, 0, m, new)
            terms.append(new * new)
        if k == 0:
            terms.append(old * old)
        return new, tuple(a + tile_sum(b) for a, b in zip(sums, terms))

    def give_back(k):
        def body(i, carry):
            to = lax.rem(member + i, GROUP)
            remote(
                field.at[k, to], back.at[k - 1, core, rows_of(block)],
                back_sem.at[0, k - 1], back_sem.at[1, k - 1], base + to,
            ).start()
            return carry

        lax.fori_loop(1, GROUP, body, 0)
        pltpu.make_async_copy(
            field.at[k, member], back.at[k - 1, core, rows_of(block)], back_sem.at[1, k - 1]
        ).start()

    def partial_faces(r):
        k = 2 * r
        for side, (m, inner) in enumerate(((0, 1), (last, last - 1))):
            new = partial(k, m, inner)
            if r < ROUNDS - 1 or side == 0:
                partial_out[r, side] = new
            put_edges(r, 1, m, new)
        begin(q_copies(r))

    def partial_rest(r):
        def body(m, carry):
            put_edges(r, 1, m, partial(2 * r, m, m - 1, m + 1))
            return carry

        lax.fori_loop(1, last, body, 0, unroll=2)
        begin(y_copies(r, 1))

    drain(field.at[0], vec_sem.at[1])
    begin(z_copies(0, 0))

    def first_edges(m, carry):
        edge_out[0, 0, 0, m] = field[0, m, 0:1]
        edge_out[0, 0, 1, m] = field[0, m, rows - 1 : rows]
        return carry

    lax.fori_loop(0, GROUP, first_edges, 0, unroll=True)
    for z, m in ((0, 0), (1, last)):
        corner_out[0, 2 * z] = field[0, m, 0:1]
        corner_out[0, 2 * z + 1] = field[0, m, rows - 1 : rows]
    begin(y_copies(0, 0))
    begin(corner_copies(0))

    def pass_on(i, carry):
        at = lax.rem(chip + i, blocks)
        plane = at * vecs + core
        drain(level.at[plane], level_in.at[at])
        remote(level.at[plane], level.at[plane], level_sem.at[1], level_sem.at[2], partner).start()
        return carry

    lax.fori_loop(0, blocks, pass_on, 0)

    def look_up_own(i, carry):
        look_up(i * vecs + core)
        return carry

    def look_up_other(i, carry):
        look_up(i * vecs + lax.rem(core + 1, vecs))
        return carry

    lax.fori_loop(0, blocks, look_up_own, 0)
    drain(level.at[pl.ds(0, blocks)], level_sem.at[2])
    lax.fori_loop(0, blocks, look_up_other, 0)

    nothing = jnp.zeros((8, lanes), jnp.float32)
    dots = [None] * (2 * LANCZOS)
    partial_faces(0)
    partial_rest(0)
    for r in range(ROUNDS):
        k = 2 * r
        final = r == ROUNDS - 1
        weight = 0.5 * scale if k == 0 else scale

        drain(edge_in.at[r, 0], edge_sem.at[1, r, 0])

        def complete(m, carry):
            field[k + 1, m, 0:8] = field[k + 1, m, 0:8] - jnp.where(sub == 0, weight * edge_in[r, 0, 0, m], 0.0)
            field[k + 1, m, rows - 8 : rows] = field[k + 1, m, rows - 8 : rows] - jnp.where(
                sub == 7, weight * edge_in[r, 0, 1, m], 0.0
            )
            return carry

        lax.fori_loop(0, GROUP, complete, 0, unroll=2)
        for side, m in ((0, 0), (1, last)):
            drain(plane_in.at[r, side], plane_sem.at[1, r, side])
            field[k + 1, m] = field[k + 1, m] - weight * plane_in[r, side]

        drain(corner_in.at[r], corner_sem.at[1, r])
        drain(edge_in.at[r, 1], edge_sem.at[1, r, 1])
        for y in range(2):
            edge[y] = edge_in[r, 1, y] - weight * edge_out[r, 0, y]
            for z, m in ((0, 0), (1, last)):
                edge[y, m] = edge[y, m] - weight * corner_in[r, 2 * z + y]

        def outside(side, m):
            drain(partial_in.at[r, side], partial_sem.at[1, r, side])
            here = field[k, m] + jnp.concatenate(
                [
                    jnp.where(sub == 0, corner_in[r, 2 * side], 0.0),
                    jnp.zeros((rows - 16, lanes), jnp.float32),
                    jnp.where(sub == 7, corner_in[r, 2 * side + 1], 0.0),
                ],
                0,
            )
            return partial_in[r, side] - weight * here

        sums = (nothing,) * 5
        if final:
            _, sums = follow(k, 0, field[k + 1, 1], sums)
            _, sums = follow(k, last, field[k + 1, last - 1] + 2.0 * outside(1, last), sums + (nothing,) * (5 - len(sums)))
        else:
            for side, m, inner in ((0, 0, 1), (1, last, last - 1)):
                new, sums = follow(k, m, field[k + 1, inner] + outside(side, m), sums + (nothing,) * (5 - len(sums)))
                put_corners(r + 1, side, new)
            begin(z_copies(r + 1, k + 2))
            begin(corner_copies(r + 1))
        sums = sums[: 3 if final else 5 if k == 0 else 4]

        def middle(m, sums):
            return follow(k, m, field[k + 1, m - 1] + field[k + 1, m + 1], sums)[1]

        if final:
            sums = lax.fori_loop(1, last, middle, sums, unroll=2)
        else:
            sums = middle(1, sums)
            sums = middle(last - 1, sums)
            partial_faces(r + 1)
            sums = lax.fori_loop(2, last - 1, middle, sums, unroll=2)
            begin(y_copies(r + 1, 0))
            partial_rest(r + 1)
        dots[2 * k + 1 : 2 * k + 4] = sums[:3]
        if not final:
            dots[2 * k + 4] = sums[3]
            give_back(r + 1)
        if k == 0:
            dots[0] = sums[4]

    lane = lax.broadcasted_iota(jnp.int32, (1, 128), 1)
    tile = jnp.zeros((1, 128), jnp.float32)
    for d, value in enumerate(dots):
        whole = jnp.sum(jnp.sum(value, axis=0, keepdims=True), axis=1, keepdims=True)
        tile = jnp.where(lane == d, whole, tile)
    mine[...] = tile
    slots[me] = tile

    def tell(i, carry):
        remote(mine, slots.at[me], sum_sem.at[0], sum_sem.at[1], lax.rem(me + i, count)).start()
        return carry

    lax.fori_loop(1, count, tell, 0)
    drain(slots.at[pl.ds(0, count - 1)], sum_sem.at[1])
    totals = [slots[v] for v in range(vecs)]
    for i in range(vecs, count):
        totals[i % vecs] = totals[i % vecs] + slots[i]
    totals = jnp.concatenate(totals, 0)
    totals = [jnp.broadcast_to(totals[:, d : d + 1], (vecs, lanes)) for d in range(len(dots))]

    nu, diag, offd = lanczos(totals, LANCZOS, jnp.sqrt)
    diag = [width * a + centre for a in diag]
    offd = [width * b for b in offd]
    third, moments = chebyshev(diag, offd, nu, centre, width)

    for k in range(RETURNED):
        drain(back.at[k], back_sem.at[1, k])
    for v in range(vecs):
        value = third[0][v : v + 1] * own[v]
        for k in range(RETURNED):
            value = value + third[k + 1][v : v + 1] * back[k, v]
        cheb[v, 0] = value

    for ref, items in ((diag_out, diag), (offd_out, offd), (moments_out, moments)):
        at = lax.broadcasted_iota(jnp.int32, ref.shape, 1)
        value = jnp.zeros(ref.shape, jnp.float32)
        for i, item in enumerate(items):
            value = jnp.where(at == i, item[:, : ref.shape[1]], value)
        ref[...] = value

    for r in range(ROUNDS):
        for copy in z_copies(r, 2 * r) + q_copies(r):
            copy.wait_send()
        for kind in range(2):
            drain(edge_out.at[r, kind], edge_sem.at[0, r, kind])
        drain(corner_out.at[r], corner_sem.at[0, r])
    drain(field.at[0, pl.ds(0, GROUP - 1)], vec_sem.at[0])
    drain(level.at[pl.ds(0, blocks - 1)], level_sem.at[0])
    drain(level.at[pl.ds(0, blocks)], level_sem.at[1])
    for k in range(RETURNED):
        drain(field.at[k + 1, pl.ds(0, GROUP - 1)], back_sem.at[0, k])
    drain(slots.at[pl.ds(0, count - 1)], sum_sem.at[0])


def shards(count, start_vectors, levels, energies):
    vecs, _, height, lanes = start_vectors.shape
    blocks = GROUP // vecs
    rows = height // blocks
    f32 = jnp.float32
    vmem = pl.BlockSpec(memory_space=pltpu.VMEM)
    anywhere = pl.BlockSpec(memory_space=pl.ANY)
    dma = pltpu.SemaphoreType.DMA
    return pl.pallas_call(
        functools.partial(kernel, count),
        out_shape=(
            jax.ShapeDtypeStruct(start_vectors.shape, f32),
            jax.ShapeDtypeStruct((vecs, LANCZOS), f32),
            jax.ShapeDtypeStruct((vecs, LANCZOS - 1), f32),
            jax.ShapeDtypeStruct((vecs, 6), f32),
        ),
        in_specs=[pl.BlockSpec(memory_space=pltpu.SMEM), anywhere, anywhere],
        out_specs=(vmem,) * 4,
        scratch_shapes=[
            pltpu.VMEM((vecs, height, lanes), f32),
            pltpu.VMEM((height, lanes), jnp.int32),
            pltpu.VMEM((LANCZOS, GROUP, rows, lanes), f32),
            pltpu.VMEM((GROUP, rows, lanes), f32),
            pltpu.VMEM((GROUP, rows, lanes), jnp.int32),
            pltpu.VMEM((RETURNED, vecs, height, lanes), f32),
            pltpu.VMEM((ROUNDS, 2, rows, lanes), f32),
            pltpu.VMEM((ROUNDS, 2, rows, lanes), f32),
            pltpu.VMEM((ROUNDS, 2, rows, lanes), f32),
            pltpu.VMEM((ROUNDS, 2, 2, GROUP, 1, lanes), f32),
            pltpu.VMEM((ROUNDS, 2, 2, GROUP, 1, lanes), f32),
            pltpu.VMEM((2, GROUP, 1, lanes), f32),
            pltpu.VMEM((ROUNDS, 4, 1, lanes), f32),
            pltpu.VMEM((ROUNDS, 4, 1, lanes), f32),
            pltpu.VMEM((count, 1, 128), f32),
            pltpu.VMEM((1, 128), f32),
            dma((2,)),
            dma((2,)),
            dma((blocks,)),
            dma((3,)),
            dma((2, ROUNDS, 2)),
            dma((2, ROUNDS, 2)),
            dma((2, ROUNDS, 2)),
            dma((2, ROUNDS)),
            dma((2, RETURNED)),
            dma((2,)),
        ],
        compiler_params=pltpu.CompilerParams(
            collective_id=0, has_side_effects=True, vmem_limit_bytes=67043328
        ),
    )(energies, start_vectors, levels)


def solution(mesh):
    in_specs = (P(None, "slab", None, None), P("slab", None, None), P())
    out_specs = (P(None, "slab", None, None), P(), P(), P())
    return jax.shard_map(
        functools.partial(shards, mesh.shape["slab"]),
        mesh=mesh, in_specs=in_specs, out_specs=out_specs, check_vma=False,
    )
```

time: 74.7 us -> 57.2 us (0.77)
  Pallas kernels: 70.1 us -> 52.7 us
    pallas_call x1, Pallas kernels: 70.1 us -> 52.7 us  [shards(): pl.pallas_call(functools.partial(kernel, count), out_shape=(jax.ShapeDtyp...]
where the time goes in v1:
time: 57.2 us; the launch traced here: 57.1 us
  Pallas kernels  52.7 us (92%)
  local copies, waits for them, and re-layouts  3.76 us (7%)
  between operations  0.65 us (1%)
    pallas_call x1, Pallas kernels, shards(): pl.pallas_call(functools.partial(kernel, count), out_shape=(jax.ShapeDtyp...  52.7 us
    unnamed x10, local copies, waits for them, and re-layouts  3.76 us

profile of v1, /device:TPU:0, one launch (start us, length us, event | category | flops | bytes accessed | tf_op | source)
XLA Modules:
  0.0 57.1 jit_solution(4232405308462814165)
XLA Ops:
  0.6 52.7 %shard_map.66 = (f32[2,1,256,256]{3,2,1,0:T(8,128)}, f32[2,8]{1,0:T(2,128)}, f32[2,7]{1,0:T(2,128)}, f32[2,6]{1,0:T(2,128)}) custom-call(f32[16]{0:T(128)} %energies.1, f32[2,1,256,256]{3,2,1,0:T(8,128)} %start.1, s32[1,256,256]{2,1,0:T(8,128)} %levels.1), custom_call_target="tpu_custom_call" | custom-call | tf_op jit(solution)/shard_map/pallas_call | solution.py:486
  53.3 0.0 copy-start.2
  53.3 1.9 %copy.11 = f32[2,1,256,256]{3,2,1,0:T(8,128)} copy(f32[2,1,256,256]{3,2,1,0:T(8,128)} %get-tuple-element.8) | data formatting | bytes 1048576
  55.2 0.0 copy-done.2
  55.2 0.0 copy-start.1
  55.2 0.6 copy.12
  55.7 0.1 copy-done.1
  55.8 0.0 copy-start
  55.8 0.6 copy.13
  56.4 0.1 copy-done
  56.5 0.6 copy.14
Async XLA Ops:
  53.3 1.9 %copy-start.2 = (f32[2,8]{1,0:T(2,128)S(1)}, f32[2,8]{1,0:T(2,128)}, u32[]{:S(2)}) copy-start(f32[2,8]{1,0:T(2,128)} %get-tuple-element.9) | copy-start | bytes 196
  55.2 0.7 %copy-start.1 = (f32[2,7]{1,0:T(2,128)S(1)}, f32[2,7]{1,0:T(2,128)}, u32[]{:S(2)}) copy-start(f32[2,7]{1,0:T(2,128)} %get-tuple-element.10) | copy-start | bytes 172
  55.8 0.7 %copy-start = (f32[2,6]{1,0:T(2,128)S(1)}, f32[2,6]{1,0:T(2,128)}, u32[]{:S(2)}) copy-start(f32[2,6]{1,0:T(2,128)} %get-tuple-element.11) | copy-start | bytes 148

commit v2 on v1

v2 whole, which is shorter than its diff:
```python
import functools

import jax
import jax.numpy as jnp
from jax import lax
from jax.experimental import pallas as pl
from jax.experimental.pallas import tpu as pltpu
from jax.sharding import PartitionSpec as P

LANCZOS = 8
ROUNDS = LANCZOS // 2
GROUP = 8
RETURNED = 3
VMEM_BYTES = 16 * 2**20


def lanczos(dots, steps, sqrt):
    norm = dots[0]
    inv_norm = 1.0 / norm
    nu = [None] * len(dots)
    nu[0] = norm * 0.0 + 1.0
    nu[1] = dots[1] * inv_norm
    for k in range(2, len(dots)):
        nu[k] = 2.0 * (dots[k] * inv_norm) - nu[k % 2]
    top = len(nu) - 1
    row, before = list(nu), None
    diag, offd = [], []
    for k in range(steps):
        if k == 0:
            alpha = row[1]
        else:
            alpha = (0.5 * row[k + 1] - offd[-1] * before[k]) / row[k]
        diag.append(alpha)
        if k == steps - 1:
            break
        new = [None] * len(nu)
        for l in range(k + 1, top - k):
            new[l] = 0.5 * (row[l + 1] + row[l - 1]) - alpha * row[l]
            if k:
                new[l] = new[l] - offd[-1] * before[l]
        beta = sqrt(new[k + 1] / (row[k] if k == 0 else 2.0 * row[k]))
        offd.append(beta)
        inv = 1.0 / beta
        before, row = row, [None if x is None else x * inv for x in new]
    return nu, diag, offd


def chebyshev(diag, offd, nu, centre, width):
    left = [None] + offd
    right = offd + [None]
    low, high = None, None
    for a, b, c in zip(diag, left, right):
        reach = b if c is None else c if b is None else b + c
        low = a - reach if low is None else jnp.minimum(low, a - reach)
        high = a + reach if high is None else jnp.maximum(high, a + reach)
    inv = 1.0 / (0.55 * (high - low))
    al = width * inv
    be = (centre - 0.5 * (high + low)) * inv
    p, q, r = 2.0 * be * be + al * al - 1.0, 4.0 * al * be, al * al
    first = [be, al]
    second = [p, q, r]
    third = [2.0 * be * p + al * q - be, 2.0 * be * q + al * (2.0 * p + r) - al, 2.0 * be * r + al * q, al * r]

    def dot(f, g):
        total = None
        for i, x in enumerate(f):
            for j, y in enumerate(g):
                term = (x * y) * (0.5 * (nu[i + j] + nu[abs(i - j)]))
                total = term if total is None else total + term
        return total

    start = [nu[0]]
    m1 = dot(start, first)
    moments = [
        m1,
        dot(start, second),
        dot(start, third),
        2.0 * dot(second, second) - 1.0,
        2.0 * dot(third, second) - m1,
        2.0 * dot(third, third) - 1.0,
    ]
    return third, moments


CORES = 2


def ring_place(member):
    chip = member // CORES
    return (chip + lax.rem(chip // 2, 2) * (1 - 2 * lax.rem(chip, 2))) * CORES + lax.rem(member, CORES)


def kernel(
    count, energies, start, levels, own, back, small,
    own_energies, own_levels, field, twice, level,
    plane_in, partial_in, partial_out, edge_in, edge_out, edge, corner_in, corner_out, slots, mine,
    load_sem, vec_sem, level_sem, plane_sem, partial_sem, edge_sem, corner_sem, back_sem, sum_sem,
):
    me = lax.axis_index("slab")
    member = lax.rem(me, GROUP)
    base = me - member
    vecs, _, height, lanes = start.shape
    rows = height // GROUP
    block = ring_place(member)
    mesh_id = pl.DeviceIdType.MESH
    ahead_base = lax.rem(base + GROUP, count)
    behind_base = lax.rem(base + count - GROUP, count)
    above = ring_place(lax.rem(block + GROUP - 1, GROUP))
    below = ring_place(lax.rem(block + 1, GROUP))
    last = GROUP - 1

    loads = [pltpu.make_async_copy(start.at[v, 0], own.at[v], load_sem.at[v]) for v in range(vecs)]
    loads.append(pltpu.make_async_copy(levels.at[0], own_levels, load_sem.at[vecs]))
    loads.append(pltpu.make_async_copy(energies, own_energies, load_sem.at[vecs + 1]))
    for copy in loads:
        copy.start()

    def remote(src, dst, send, recv, to):
        return pltpu.make_async_remote_copy(
            src_ref=src, dst_ref=dst, send_sem=send, recv_sem=recv, device_id=(to,), device_id_type=mesh_id
        )

    def drain(ref, sem):
        pltpu.make_async_copy(ref, ref, sem).wait()

    barrier = pltpu.get_barrier_semaphore()

    def greet(to):
        pl.semaphore_signal(barrier, inc=1, device_id=(to,), device_id_type=mesh_id)

    def greet_member(i, carry):
        greet(base + lax.rem(member + i, GROUP))
        return carry

    greet(behind_base + member)
    greet(ahead_base + member)
    lax.fori_loop(1, GROUP, greet_member, 0)
    pl.semaphore_wait(barrier, GROUP - 1 + 2)

    def rows_of(at):
        return pl.ds(pl.multiple_of(at * rows, 8), rows)

    def scatter(src, dst, sem):
        def body(i, carry):
            to = lax.rem(member + i, GROUP)
            remote(src.at[rows_of(ring_place(to))], dst.at[member], sem.at[0], sem.at[1], base + to).start()
            return carry

        lax.fori_loop(1, GROUP, body, 0)
        pltpu.make_async_copy(src.at[rows_of(block)], dst.at[member], sem.at[1]).start()

    for v in range(vecs):
        loads[v].wait()
        scatter(own.at[v], field.at[v, 0], vec_sem.at[v])
        if v == 0:
            loads[vecs].wait()
            scatter(own_levels, level, level_sem)

    loads[vecs + 1].wait()
    values = [own_energies[i] for i in range(energies.shape[0])]
    share = 1.0 / len(values)

    def total(terms):
        return sum(terms[1:], terms[0])

    mean = total(values) * share
    apart = [x - mean for x in values]
    square = [x * x for x in apart]
    second = total(square) * share + 6.0
    cube = total([x * y for x, y in zip(square, apart)]) * share
    fourth = total([x * x for x in square]) * share + 24.0 * (second - 6.0) + 90.0
    inv_second = 1.0 / jnp.full((1, lanes), second, jnp.float32)
    skew = cube * inv_second
    centre = mean + 0.5 * skew
    width = jnp.sqrt(2.0 * (fourth * inv_second - skew * skew))
    scale = 2.0 / width

    sub = lax.broadcasted_iota(jnp.int32, (8, lanes), 0)
    zero_row = jnp.zeros((1, lanes), jnp.float32)

    def look_up(m, carry):
        ids = level[m]
        found = [jnp.full(ids.shape, x, jnp.float32) for x in values]
        bit = 1
        while len(found) > 1:
            odd = (ids & bit) != 0
            found = [
                found[i] if i + 1 == len(found) else jnp.where(odd, found[i + 1], found[i])
                for i in range(0, len(found), 2)
            ]
            bit *= 2
        twice[m] = (found[0] - centre) * scale
        return carry

    def z_copies(v, r):
        return [
            remote(
                field.at[v, 2 * r, m], plane_in.at[v, r, 1 - z],
                plane_sem.at[0, v, r, z], plane_sem.at[1, v, r, 1 - z], side + member,
            )
            for z, m, side in ((0, 0, behind_base), (1, last, ahead_base))
        ]

    def q_copies(v, r):
        sides = ((0, behind_base), (1, ahead_base))
        return [
            remote(
                partial_out.at[v, r, z], partial_in.at[v, r, 1 - z],
                partial_sem.at[0, v, r, z], partial_sem.at[1, v, r, 1 - z], side + member,
            )
            for z, side in (sides[:1] if r == ROUNDS - 1 else sides)
        ]

    def y_copies(v, r, kind):
        return [
            remote(
                edge_out.at[v, r, kind, y], edge_in.at[v, r, kind, 1 - y],
                edge_sem.at[0, v, r, kind], edge_sem.at[1, v, r, kind], base + place,
            )
            for y, place in ((0, above), (1, below))
        ]

    def corner_copies(v, r):
        return [
            remote(
                corner_out.at[v, r, 2 * z + y], corner_in.at[v, r, 2 * (1 - z) + (1 - y)],
                corner_sem.at[0, v, r], corner_sem.at[1, v, r], side + place,
            )
            for z, side in ((0, behind_base), (1, ahead_base))
            for y, place in ((0, above), (1, below))
        ]

    def begin(copies):
        for copy in copies:
            copy.start()

    def put_corners(v, r, z, value):
        corner_out[v, r, 2 * z] = value[0:1]
        corner_out[v, r, 2 * z + 1] = value[rows - 1 : rows]

    def put_edges(v, r, kind, m, value):
        edge_out[v, r, kind, 0, m] = value[0:1]
        edge_out[v, r, kind, 1, m] = value[rows - 1 : rows]

    def around(here, top, bottom):
        up, down = pltpu.roll(here, 1, 0), pltpu.roll(here, rows - 1, 0)
        first = jnp.where(sub == 0, top, up[0:8])
        final = jnp.where(sub == 7, bottom, down[rows - 8 :])
        near = jnp.concatenate([first, up[8:]], 0) + jnp.concatenate([down[: rows - 8], final], 0)
        return near + (pltpu.roll(here, 1, 1) + pltpu.roll(here, lanes - 1, 1))

    def partial(v, k, m, *beside):
        here = field[v, k, m]
        near = around(here, zero_row, zero_row)
        for plane in beside:
            near = near + field[v, k, plane]
        new = twice[m] * here - scale * near
        new = 0.5 * new if k == 0 else new - field[v, k - 1, m]
        field[v, k + 1, m] = new
        return new

    def tile_sum(x):
        parts = [x[i : i + 8] for i in range(0, rows, 8)]
        while len(parts) > 1:
            parts = [a + b for a, b in zip(parts[::2], parts[1::2])]
        return parts[0]

    def follow(v, k, m, near, sums):
        here, old = field[v, k + 1, m], field[v, k, m]
        near = near + around(here, edge[0, m], edge[1, m])
        new = twice[m] * here - scale * near - old
        terms = [old * here, here * here, here * new]
        if k + 2 < LANCZOS:
            field[v, k + 2, m] = new
            put_edges(v, k // 2 + 1, 0, m, new)
            terms.append(new * new)
        if k == 0:
            terms.append(old * old)
        return new, tuple(a + tile_sum(b) for a, b in zip(sums, terms))

    def give_back(v, k):
        send, recv = back_sem.at[0, v, k - 1], back_sem.at[1, v, k - 1]

        def body(i, carry):
            to = lax.rem(member + i, GROUP)
            remote(field.at[v, k, to], back.at[k - 1, v, rows_of(block)], send, recv, base + to).start()
            return carry

        lax.fori_loop(1, GROUP, body, 0)
        pltpu.make_async_copy(field.at[v, k, member], back.at[k - 1, v, rows_of(block)], recv).start()

    def partial_faces(v, r):
        for side, (m, inner) in enumerate(((0, 1), (last, last - 1))):
            new = partial(v, 2 * r, m, inner)
            if r < ROUNDS - 1 or side == 0:
                partial_out[v, r, side] = new
            put_edges(v, r, 1, m, new)
        begin(q_copies(v, r))

    def partial_rest(v, r):
        def body(m, carry):
            put_edges(v, r, 1, m, partial(v, 2 * r, m, m - 1, m + 1))
            return carry

        lax.fori_loop(1, last, body, 0, unroll=2)
        begin(y_copies(v, r, 1))

    def arrive(v):
        drain(field.at[v, 0], vec_sem.at[v, 1])
        for z, m in ((0, 0), (1, last)):
            corner_out[v, 0, 2 * z] = field[v, 0, m, 0:1]
            corner_out[v, 0, 2 * z + 1] = field[v, 0, m, rows - 1 : rows]
        begin(corner_copies(v, 0))
        begin(z_copies(v, 0))

        def edges(m, carry):
            edge_out[v, 0, 0, 0, m] = field[v, 0, m, 0:1]
            edge_out[v, 0, 0, 1, m] = field[v, 0, m, rows - 1 : rows]
            return carry

        lax.fori_loop(0, GROUP, edges, 0, unroll=True)
        begin(y_copies(v, 0, 0))

    nothing = jnp.zeros((8, lanes), jnp.float32)
    dots = [[None] * (2 * LANCZOS) for v in range(vecs)]

    def advance(v, r):
        k = 2 * r
        final = r == ROUNDS - 1
        weight = 0.5 * scale if k == 0 else scale

        drain(edge_in.at[v, r, 0], edge_sem.at[1, v, r, 0])

        def complete(m, carry):
            field[v, k + 1, m, 0:8] = field[v, k + 1, m, 0:8] - jnp.where(
                sub == 0, weight * edge_in[v, r, 0, 0, m], 0.0
            )
            field[v, k + 1, m, rows - 8 : rows] = field[v, k + 1, m, rows - 8 : rows] - jnp.where(
                sub == 7, weight * edge_in[v, r, 0, 1, m], 0.0
            )
            return carry

        lax.fori_loop(0, GROUP, complete, 0, unroll=2)
        for side, m in ((0, 0), (1, last)):
            drain(plane_in.at[v, r, side], plane_sem.at[1, v, r, side])
            field[v, k + 1, m] = field[v, k + 1, m] - weight * plane_in[v, r, side]
        if r == 0:
            give_back(v, 1)

        drain(edge_in.at[v, r, 1], edge_sem.at[1, v, r, 1])
        if r in (1, 2):
            give_back(v, r + 1)
        for y in range(2):
            edge[y] = edge_in[v, r, 1, y] - weight * edge_out[v, r, 0, y]

        def outside(side, m):
            drain(partial_in.at[v, r, side], partial_sem.at[1, v, r, side])
            here = field[v, k, m] + jnp.concatenate(
                [
                    jnp.where(sub == 0, corner_in[v, r, 2 * side], 0.0),
                    jnp.zeros((rows - 16, lanes), jnp.float32),
                    jnp.where(sub == 7, corner_in[v, r, 2 * side + 1], 0.0),
                ],
                0,
            )
            return partial_in[v, r, side] - weight * here

        def middle(m, sums):
            return follow(v, k, m, field[v, k + 1, m - 1] + field[v, k + 1, m + 1], sums)[1]

        sums = (nothing,) * (3 if final else 5 if k == 0 else 4)
        sums = lax.fori_loop(1, last, middle, sums, unroll=2)
        drain(corner_in.at[v, r], corner_sem.at[1, v, r])
        for y in range(2):
            for z, m in ((0, 0), (1, last)):
                edge[y, m] = edge[y, m] - weight * corner_in[v, r, 2 * z + y]
        if final:
            _, sums = follow(v, k, 0, field[v, k + 1, 1], sums)
            _, sums = follow(v, k, last, field[v, k + 1, last - 1] + 2.0 * outside(1, last), sums)
        else:
            for side, m, inner in ((0, 0, 1), (1, last, last - 1)):
                new, sums = follow(v, k, m, field[v, k + 1, inner] + outside(side, m), sums)
                put_corners(v, r + 1, side, new)
            begin(corner_copies(v, r + 1))
            begin(z_copies(v, r + 1))
            begin(y_copies(v, r + 1, 0))
            partial_faces(v, r + 1)
            partial_rest(v, r + 1)
        dots[v][2 * k + 1 : 2 * k + 4] = sums[:3]
        if not final:
            dots[v][2 * k + 4] = sums[3]
        if k == 0:
            dots[v][0] = sums[4]

    arrive(0)
    drain(level, level_sem.at[1])
    lax.fori_loop(0, GROUP, look_up, 0)
    for v in range(vecs):
        if v:
            arrive(v)
        partial_faces(v, 0)
        partial_rest(v, 0)
    for r in range(ROUNDS):
        for v in range(vecs):
            advance(v, r)

    lane = lax.broadcasted_iota(jnp.int32, (1, 128), 1)
    tile = jnp.zeros((1, 128), jnp.float32)
    for v in range(vecs):
        for d, value in enumerate(dots[v]):
            whole = jnp.sum(jnp.sum(value, axis=0, keepdims=True), axis=1, keepdims=True)
            tile = jnp.where(lane == v * len(dots[v]) + d, whole, tile)
    mine[...] = tile
    slots[me] = tile

    def tell(i, carry):
        remote(mine, slots.at[me], sum_sem.at[0], sum_sem.at[1], lax.rem(me + i, count)).start()
        return carry

    lax.fori_loop(1, count, tell, 0)
    drain(slots.at[pl.ds(0, count - 1)], sum_sem.at[1])
    parts = [slots[i] for i in range(count)]
    while len(parts) > 1:
        parts = [a + b for a, b in zip(parts[::2], parts[1::2])] + parts[len(parts) // 2 * 2 :]

    def spread(d):
        at = [v * 2 * LANCZOS + d for v in range(vecs)]
        return jnp.concatenate([jnp.broadcast_to(parts[0][:, i : i + 1], (1, 128)) for i in at], 0)

    nu, diag, offd = lanczos([spread(d) for d in range(2 * LANCZOS)], LANCZOS, jnp.sqrt)
    centre, width = centre[:, :128], width[:, :128]
    diag = [width * a + centre for a in diag]
    offd = [width * b for b in offd]
    third, moments = chebyshev(diag, offd, nu, centre, width)

    at = lax.broadcasted_iota(jnp.int32, small.shape[1:], 1)
    for n, items in enumerate((third, diag, offd, moments)):
        value = jnp.zeros(small.shape[1:], jnp.float32)
        for i, item in enumerate(items):
            value = jnp.where(at == i, item, value)
        small[n] = value

    for v in range(vecs):
        for k in range(RETURNED):
            drain(back.at[k, v], back_sem.at[1, v, k])
            drain(field.at[v, k + 1, pl.ds(0, GROUP - 1)], back_sem.at[0, v, k])
        for r in range(ROUNDS):
            for copy in z_copies(v, r) + q_copies(v, r):
                copy.wait_send()
            for kind in range(2):
                drain(edge_out.at[v, r, kind], edge_sem.at[0, v, r, kind])
            drain(corner_out.at[v, r], corner_sem.at[0, v, r])
        drain(field.at[v, 0, pl.ds(0, GROUP - 1)], vec_sem.at[v, 0])
    drain(level.at[pl.ds(0, GROUP - 1)], level_sem.at[0])
    drain(slots.at[pl.ds(0, count - 1)], sum_sem.at[0])


def finish(own, back, small, cheb, diag, offd, moments):
    vecs, lanes = own.shape[0], own.shape[2]
    for v in range(vecs):
        third = [jnp.broadcast_to(small[0, v : v + 1, k : k + 1], (1, lanes)) for k in range(RETURNED + 1)]
        value = third[0] * own[v]
        for k in range(RETURNED):
            value = value + third[k + 1] * back[k, v]
        cheb[v, 0] = value
    for n, ref in enumerate((diag, offd, moments)):
        ref[...] = small[n + 1, :, : ref.shape[1]]


def shards(count, start_vectors, levels, energies):
    vecs, _, height, lanes = start_vectors.shape
    rows = height // GROUP
    f32 = jnp.float32
    vmem = pl.BlockSpec(memory_space=pltpu.VMEM)
    dma = pltpu.SemaphoreType.DMA
    kept = pl.pallas_call(
        functools.partial(kernel, count),
        out_shape=(
            jax.ShapeDtypeStruct((vecs, height, lanes), f32),
            jax.ShapeDtypeStruct((RETURNED, vecs, height, lanes), f32),
            jax.ShapeDtypeStruct((4, vecs, 128), f32),
        ),
        in_specs=[pl.BlockSpec(memory_space=pltpu.HBM)] * 3,
        out_specs=(vmem,) * 3,
        scratch_shapes=[
            pltpu.SMEM(energies.shape, f32),
            pltpu.VMEM((height, lanes), jnp.int32),
            pltpu.VMEM((vecs, LANCZOS, GROUP, rows, lanes), f32),
            pltpu.VMEM((GROUP, rows, lanes), f32),
            pltpu.VMEM((GROUP, rows, lanes), jnp.int32),
            pltpu.VMEM((vecs, ROUNDS, 2, rows, lanes), f32),
            pltpu.VMEM((vecs, ROUNDS, 2, rows, lanes), f32),
            pltpu.VMEM((vecs, ROUNDS, 2, rows, lanes), f32),
            pltpu.VMEM((vecs, ROUNDS, 2, 2, GROUP, 1, lanes), f32),
            pltpu.VMEM((vecs, ROUNDS, 2, 2, GROUP, 1, lanes), f32),
            pltpu.VMEM((2, GROUP, 1, lanes), f32),
            pltpu.VMEM((vecs, ROUNDS, 4, 1, lanes), f32),
            pltpu.VMEM((vecs, ROUNDS, 4, 1, lanes), f32),
            pltpu.VMEM((count, 1, 128), f32),
            pltpu.VMEM((1, 128), f32),
            dma((vecs + 2,)),
            dma((vecs, 2)),
            dma((2,)),
            dma((2, vecs, ROUNDS, 2)),
            dma((2, vecs, ROUNDS, 2)),
            dma((2, vecs, ROUNDS, 2)),
            dma((2, vecs, ROUNDS)),
            dma((2, vecs, RETURNED)),
            dma((2,)),
        ],
        compiler_params=pltpu.CompilerParams(
            collective_id=0, has_side_effects=True, vmem_limit_bytes=VMEM_BYTES
        ),
    )(*(pltpu.with_memory_space_constraint(x, pltpu.HBM) for x in (energies, start_vectors, levels)))
    return pl.pallas_call(
        finish,
        out_shape=(
            jax.ShapeDtypeStruct(start_vectors.shape, f32),
            jax.ShapeDtypeStruct((vecs, LANCZOS), f32),
            jax.ShapeDtypeStruct((vecs, LANCZOS - 1), f32),
            jax.ShapeDtypeStruct((vecs, 6), f32),
        ),
        in_specs=[vmem] * 3,
        out_specs=(vmem,) * 4,
        compiler_params=pltpu.CompilerParams(vmem_limit_bytes=VMEM_BYTES),
    )(*kept)


def solution(mesh):
    in_specs = (P(None, "slab", None, None), P("slab", None, None), P())
    out_specs = (P(None, "slab", None, None), P(), P(), P())
    return jax.shard_map(
        functools.partial(shards, mesh.shape["slab"]),
        mesh=mesh, in_specs=in_specs, out_specs=out_specs, check_vma=False,
    )
```

time: 57.2 us -> 47.1 us (0.82)
  Pallas kernels: 52.7 us -> 46.3 us
  local copies, waits for them, and re-layouts: 3.76 us -> 0 us
    pallas_call x1, Pallas kernels: 52.7 us -> 45.2 us  [shards(): pl.pallas_call(functools.partial(kernel, count), out_shape=(jax.ShapeDtyp...]
    unnamed x10 -> x0, local copies, waits for them, and re-layouts: 3.76 us -> none
    pallas_call x0 -> x1, Pallas kernels: none -> 1.11 us  [shards(): pl.pallas_call(finish, out_shape=(jax.ShapeDtypeStruct(start_vectors.shap...]
where the time goes in v2:
time: 47.1 us; the launch traced here: 46.9 us
  Pallas kernels  46.3 us (98%)
  between operations  0.64 us (1%)
    pallas_call x1, Pallas kernels, shards(): pl.pallas_call(functools.partial(kernel, count), out_shape=(jax.ShapeDtyp...  45.2 us
    pallas_call x1, Pallas kernels, shards(): pl.pallas_call(finish, out_shape=(jax.ShapeDtypeStruct(start_vectors.shap...  1.11 us

profile of v2, /device:TPU:0, one launch (start us, length us, event | category | flops | bytes accessed | tf_op | source)
XLA Modules:
  0.0 46.9 jit_solution(8620991258172141468)
XLA Ops:
  0.6 45.2 %shard_map.66 = (f32[2,256,256]{2,1,0:T(8,128)S(1)}, f32[3,2,256,256]{3,2,1,0:T(8,128)S(1)}, f32[4,2,128]{2,1,0:T(2,128)S(1)}) custom-call(f32[16]{0:T(128)} %energies.1, f32[2,1,256,256]{3,2,1,0:T(8,128)} %start.1, s32[1,256,256]{2,1,0:T(8,128)} %levels.1), custom_call_target="tpu_custom_call" | custom-call | tf_op jit(solution)/shard_map/pallas_call | solution.py:476
  45.8 1.1 %shard_map.67 = (f32[2,1,256,256]{3,2,1,0:T(8,128)}, f32[2,8]{1,0:T(2,128)}, f32[2,7]{1,0:T(2,128)}, f32[2,6]{1,0:T(2,128)}) custom-call(f32[2,256,256]{2,1,0:T(8,128)S(1)} %get-tuple-element.7.own, f32[3,2,256,256]{3,2,1,0:T(8,128)S(1)} %get-tuple-element.8.back, f32[4,2,128]{2,1,0:T(2,128)S(1)} %get-tuple-element.9.small), custom_call_target="tpu_custom_call" | custom-call | tf_op jit(solution)/shard_map/pallas_call | solution.py:515

commit v3 on v2

--- a/solution.py
+++ b/solution.py
@@ -15,33 +15,27 @@
 
 
 def lanczos(dots, steps, sqrt):
-    norm = dots[0]
-    inv_norm = 1.0 / norm
-    nu = [None] * len(dots)
-    nu[0] = norm * 0.0 + 1.0
-    nu[1] = dots[1] * inv_norm
+    inv_norm = 1.0 / dots[0]
+    nu = [dots[0] * 0.0 + 1.0, dots[1] * inv_norm]
     for k in range(2, len(dots)):
-        nu[k] = 2.0 * (dots[k] * inv_norm) - nu[k % 2]
-    top = len(nu) - 1
-    row, before = list(nu), None
+        nu.append(2.0 * (dots[k] * inv_norm) - nu[k % 2])
+    row, before = dict(enumerate(nu)), None
     diag, offd = [], []
     for k in range(steps):
-        if k == 0:
-            alpha = row[1]
-        else:
-            alpha = (0.5 * row[k + 1] - offd[-1] * before[k]) / row[k]
+        factor = 1.0 if k == 1 else 0.5
+        alpha = row[1] if k == 0 else 0.5 * row[k + 1] - factor * before[k]
         diag.append(alpha)
         if k == steps - 1:
             break
-        new = [None] * len(nu)
-        for l in range(k + 1, top - k):
-            new[l] = 0.5 * (row[l + 1] + row[l - 1]) - alpha * row[l]
+        new = {}
+        for l in range(k + 1, 2 * steps - 1 - k):
+            new[l] = 0.5 * (row[l + 1] + (row[l - 1] if l - 1 > k else 1.0)) - alpha * row[l]
             if k:
-                new[l] = new[l] - offd[-1] * before[l]
-        beta = sqrt(new[k + 1] / (row[k] if k == 0 else 2.0 * row[k]))
-        offd.append(beta)
-        inv = 1.0 / beta
-        before, row = row, [None if x is None else x * inv for x in new]
+                new[l] = new[l] - factor * before[l]
+        first = new.pop(k + 1)
+        offd.append(sqrt(first if k == 0 else 0.5 * first))
+        inv = 1.0 / first
+        before, row = row, {l: x * inv for l, x in new.items()}
     return nu, diag, offd
 
 
@@ -94,7 +88,7 @@
     count, energies, start, levels, own, back, small,
     own_energies, own_levels, field, twice, level,
     plane_in, partial_in, partial_out, edge_in, edge_out, edge, corner_in, corner_out, slots, mine,
-    load_sem, vec_sem, level_sem, plane_sem, partial_sem, edge_sem, corner_sem, back_sem, sum_sem,
+    load_sem, vec_sem, level_sem, plane_sem, partial_sem, edge_sem, corner_sem, back_sem, sum_sem, sent,
 ):
     me = lax.axis_index("slab")
     member = lax.rem(me, GROUP)
@@ -140,21 +134,21 @@
     def rows_of(at):
         return pl.ds(pl.multiple_of(at * rows, 8), rows)
 
-    def scatter(src, dst, sem):
+    def scatter(src, dst, send, recv):
         def body(i, carry):
             to = lax.rem(member + i, GROUP)
-            remote(src.at[rows_of(ring_place(to))], dst.at[member], sem.at[0], sem.at[1], base + to).start()
+            remote(src.at[rows_of(ring_place(to))], dst.at[member], send, recv, base + to).start()
             return carry
 
         lax.fori_loop(1, GROUP, body, 0)
-        pltpu.make_async_copy(src.at[rows_of(block)], dst.at[member], sem.at[1]).start()
+        pltpu.make_async_copy(src.at[rows_of(block)], dst.at[member], recv).start()
 
     for v in range(vecs):
         loads[v].wait()
-        scatter(own.at[v], field.at[v, 0], vec_sem.at[v])
+        scatter(own.at[v], field.at[v, 0], sent.at[4], vec_sem.at[v])
         if v == 0:
             loads[vecs].wait()
-            scatter(own_levels, level, level_sem)
+            scatter(own_levels, level, sent.at[5], level_sem)
 
     loads[vecs + 1].wait()
     values = [own_energies[i] for i in range(energies.shape[0])]
@@ -192,30 +186,33 @@
         twice[m] = (found[0] - centre) * scale
         return carry
 
+    def sides():
+        flip = me // (count - GROUP)
+        return ((flip, jnp.where(flip == 1, ahead_base, behind_base)), (1 - flip, jnp.where(flip == 1, behind_base, ahead_base)))
+
     def z_copies(v, r):
         return [
             remote(
-                field.at[v, 2 * r, m], plane_in.at[v, r, 1 - z],
-                plane_sem.at[0, v, r, z], plane_sem.at[1, v, r, 1 - z], side + member,
-            )
-            for z, m, side in ((0, 0, behind_base), (1, last, ahead_base))
+                field.at[v, 2 * r, z * last], plane_in.at[v, r, 1 - z],
+                sent.at[0], plane_sem.at[v, r % 2], side + member,
+            )
+            for z, side in sides()
         ]
 
     def q_copies(v, r):
-        sides = ((0, behind_base), (1, ahead_base))
         return [
             remote(
                 partial_out.at[v, r, z], partial_in.at[v, r, 1 - z],
-                partial_sem.at[0, v, r, z], partial_sem.at[1, v, r, 1 - z], side + member,
-            )
-            for z, side in (sides[:1] if r == ROUNDS - 1 else sides)
+                sent.at[1], partial_sem.at[v, r % 2], side + member,
+            )
+            for z, side in (((0, behind_base),) if r == ROUNDS - 1 else sides())
         ]
 
     def y_copies(v, r, kind):
         return [
             remote(
                 edge_out.at[v, r, kind, y], edge_in.at[v, r, kind, 1 - y],
-                edge_sem.at[0, v, r, kind], edge_sem.at[1, v, r, kind], base + place,
+                sent.at[2], edge_sem.at[v, r % 2, kind], base + place,
             )
             for y, place in ((0, above), (1, below))
         ]
@@ -224,7 +221,7 @@
         return [
             remote(
                 corner_out.at[v, r, 2 * z + y], corner_in.at[v, r, 2 * (1 - z) + (1 - y)],
-                corner_sem.at[0, v, r], corner_sem.at[1, v, r], side + place,
+                sent.at[3], corner_sem.at[v, r % 2], side + place,
             )
             for z, side in ((0, behind_base), (1, ahead_base))
             for y, place in ((0, above), (1, below))
@@ -279,15 +276,13 @@
         return new, tuple(a + tile_sum(b) for a, b in zip(sums, terms))
 
     def give_back(v, k):
-        send, recv = back_sem.at[0, v, k - 1], back_sem.at[1, v, k - 1]
-
         def body(i, carry):
             to = lax.rem(member + i, GROUP)
-            remote(field.at[v, k, to], back.at[k - 1, v, rows_of(block)], send, recv, base + to).start()
+            remote(field.at[v, k, to], back.at[k - 1, v, rows_of(block)], sent.at[6], back_sem, base + to).start()
             return carry
 
         lax.fori_loop(1, GROUP, body, 0)
-        pltpu.make_async_copy(field.at[v, k, member], back.at[k - 1, v, rows_of(block)], recv).start()
+        pltpu.make_async_copy(field.at[v, k, member], back.at[k - 1, v, rows_of(block)], back_sem).start()
 
     def partial_faces(v, r):
         for side, (m, inner) in enumerate(((0, 1), (last, last - 1))):
@@ -306,7 +301,7 @@
         begin(y_copies(v, r, 1))
 
     def arrive(v):
-        drain(field.at[v, 0], vec_sem.at[v, 1])
+        drain(field.at[v, 0], vec_sem.at[v])
         for z, m in ((0, 0), (1, last)):
             corner_out[v, 0, 2 * z] = field[v, 0, m, 0:1]
             corner_out[v, 0, 2 * z + 1] = field[v, 0, m, rows - 1 : rows]
@@ -329,7 +324,7 @@
         final = r == ROUNDS - 1
         weight = 0.5 * scale if k == 0 else scale
 
-        drain(edge_in.at[v, r, 0], edge_sem.at[1, v, r, 0])
+        drain(edge_in.at[v, r, 0], edge_sem.at[v, r % 2, 0])
 
         def complete(m, carry):
             field[v, k + 1, m, 0:8] = field[v, k + 1, m, 0:8] - jnp.where(
@@ -341,20 +336,19 @@
             return carry
 
         lax.fori_loop(0, GROUP, complete, 0, unroll=2)
+        drain(plane_in.at[v, r], plane_sem.at[v, r % 2])
         for side, m in ((0, 0), (1, last)):
-            drain(plane_in.at[v, r, side], plane_sem.at[1, v, r, side])
             field[v, k + 1, m] = field[v, k + 1, m] - weight * plane_in[v, r, side]
         if r == 0:
             give_back(v, 1)
 
-        drain(edge_in.at[v, r, 1], edge_sem.at[1, v, r, 1])
+        drain(edge_in.at[v, r, 1], edge_sem.at[v, r % 2, 1])
         if r in (1, 2):
             give_back(v, r + 1)
         for y in range(2):
             edge[y] = edge_in[v, r, 1, y] - weight * edge_out[v, r, 0, y]
 
         def outside(side, m):
-            drain(partial_in.at[v, r, side], partial_sem.at[1, v, r, side])
             here = field[v, k, m] + jnp.concatenate(
                 [
                     jnp.where(sub == 0, corner_in[v, r, 2 * side], 0.0),
@@ -370,14 +364,17 @@
 
         sums = (nothing,) * (3 if final else 5 if k == 0 else 4)
         sums = lax.fori_loop(1, last, middle, sums, unroll=2)
-        drain(corner_in.at[v, r], corner_sem.at[1, v, r])
+        drain(corner_in.at[v, r], corner_sem.at[v, r % 2])
         for y in range(2):
             for z, m in ((0, 0), (1, last)):
                 edge[y, m] = edge[y, m] - weight * corner_in[v, r, 2 * z + y]
+        came = partial_in.at[v, r, 1] if final else partial_in.at[v, r]
         if final:
             _, sums = follow(v, k, 0, field[v, k + 1, 1], sums)
+            drain(came, partial_sem.at[v, r % 2])
             _, sums = follow(v, k, last, field[v, k + 1, last - 1] + 2.0 * outside(1, last), sums)
         else:
+            drain(came, partial_sem.at[v, r % 2])
             for side, m, inner in ((0, 0, 1), (1, last, last - 1)):
                 new, sums = follow(v, k, m, field[v, k + 1, inner] + outside(side, m), sums)
                 put_corners(v, r + 1, side, new)
@@ -393,7 +390,7 @@
             dots[v][0] = sums[4]
 
     arrive(0)
-    drain(level, level_sem.at[1])
+    drain(level, level_sem)
     lax.fori_loop(0, GROUP, look_up, 0)
     for v in range(vecs):
         if v:
@@ -417,7 +414,17 @@
         remote(mine, slots.at[me], sum_sem.at[0], sum_sem.at[1], lax.rem(me + i, count)).start()
         return carry
 
-    lax.fori_loop(1, count, tell, 0)
+    lax.fori_loop(1, count, tell, 0, unroll=8)
+    others = pl.ds(0, GROUP - 1)
+    drain(plane_in, sent.at[0])
+    drain(field.at[:, 0, pl.ds(0, 2 * ROUNDS - 1)], sent.at[1])
+    drain(edge_out, sent.at[2])
+    drain(corner_out, sent.at[3])
+    drain(field.at[:, 0, others], sent.at[4])
+    drain(level.at[others], sent.at[5])
+    drain(field.at[:, pl.ds(1, RETURNED), others], sent.at[6])
+    drain(back, back_sem)
+    drain(slots.at[pl.ds(0, count - 1)], sum_sem.at[0])
     drain(slots.at[pl.ds(0, count - 1)], sum_sem.at[1])
     parts = [slots[i] for i in range(count)]
     while len(parts) > 1:
@@ -439,20 +446,6 @@
         for i, item in enumerate(items):
             value = jnp.where(at == i, item, value)
         small[n] = value
-
-    for v in range(vecs):
-        for k in range(RETURNED):
-            drain(back.at[k, v], back_sem.at[1, v, k])
-            drain(field.at[v, k + 1, pl.ds(0, GROUP - 1)], back_sem.at[0, v, k])
-        for r in range(ROUNDS):
-            for copy in z_copies(v, r) + q_copies(v, r):
-                copy.wait_send()
-            for kind in range(2):
-                drain(edge_out.at[v, r, kind], edge_sem.at[0, v, r, kind])
-            drain(corner_out.at[v, r], corner_sem.at[0, v, r])
-        drain(field.at[v, 0, pl.ds(0, GROUP - 1)], vec_sem.at[v, 0])
-    drain(level.at[pl.ds(0, GROUP - 1)], level_sem.at[0])
-    drain(slots.at[pl.ds(0, count - 1)], sum_sem.at[0])
 
 
 def finish(own, back, small, cheb, diag, offd, moments):
@@ -499,14 +492,15 @@
             pltpu.VMEM((count, 1, 128), f32),
             pltpu.VMEM((1, 128), f32),
             dma((vecs + 2,)),
+            dma((vecs,)),
+            dma,
             dma((vecs, 2)),
+            dma((vecs, 2)),
+            dma((vecs, 2, 2)),
+            dma((vecs, 2)),
+            dma,
             dma((2,)),
-            dma((2, vecs, ROUNDS, 2)),
-            dma((2, vecs, ROUNDS, 2)),
-            dma((2, vecs, ROUNDS, 2)),
-            dma((2, vecs, ROUNDS)),
-            dma((2, vecs, RETURNED)),
-            dma((2,)),
+            dma((7,)),
         ],
         compiler_params=pltpu.CompilerParams(
             collective_id=0, has_side_effects=True, vmem_limit_bytes=VMEM_BYTES

time: 47.1 us -> 45.2 us (0.960)
  Pallas kernels: 46.3 us -> 44.4 us
    pallas_call x1, Pallas kernels: 45.2 us -> 43.3 us  [shards(): pl.pallas_call(functools.partial(kernel, count), out_shape=(jax.ShapeDtyp...]
where the time goes in v3:
time: 45.2 us; the launch traced here: 45.1 us
  Pallas kernels  44.4 us (98%)
  between operations  0.64 us (1%)
    pallas_call x1, Pallas kernels, shards(): pl.pallas_call(functools.partial(kernel, count), out_shape=(jax.ShapeDtyp...  43.3 us
    pallas_call x1, Pallas kernels, shards(): pl.pallas_call(finish, out_shape=(jax.ShapeDtypeStruct(start_vectors.shap...  1.11 us

profile of v3, /device:TPU:0, one launch (start us, length us, event | category | flops | bytes accessed | tf_op | source)
XLA Modules:
  0.0 45.1 jit_solution(2962076039463110136)
XLA Ops:
  0.6 43.3 %shard_map.66 = (f32[2,256,256]{2,1,0:T(8,128)S(1)}, f32[3,2,256,256]{3,2,1,0:T(8,128)S(1)}, f32[4,2,128]{2,1,0:T(2,128)S(1)}) custom-call(f32[16]{0:T(128)} %energies.1, f32[2,1,256,256]{3,2,1,0:T(8,128)} %start.1, s32[1,256,256]{2,1,0:T(8,128)} %levels.1), custom_call_target="tpu_custom_call" | custom-call | tf_op jit(solution)/shard_map/pallas_call | solution.py:469
  44.0 1.1 %shard_map.67 = (f32[2,1,256,256]{3,2,1,0:T(8,128)}, f32[2,8]{1,0:T(2,128)}, f32[2,7]{1,0:T(2,128)}, f32[2,6]{1,0:T(2,128)}) custom-call(f32[2,256,256]{2,1,0:T(8,128)S(1)} %get-tuple-element.7.own, f32[3,2,256,256]{3,2,1,0:T(8,128)S(1)} %get-tuple-element.8.back, f32[4,2,128]{2,1,0:T(2,128)S(1)} %get-tuple-element.9.small), custom_call_target="tpu_custom_call" | custom-call | tf_op jit(solution)/shard_map/pallas_call | solution.py:509

commit v4 on v3

--- a/solution.py
+++ b/solution.py
@@ -143,12 +143,25 @@
         lax.fori_loop(1, GROUP, body, 0)
         pltpu.make_async_copy(src.at[rows_of(block)], dst.at[member], recv).start()
 
-    for v in range(vecs):
+    others = pl.ds(0, GROUP - 1)
+    mate = (member == 1) | (member == last - 1)
+
+    inner = jnp.where((member == 0) | (member == last), 0, 1)
+
+    def scatter_vec(v):
+        scatter(own.at[v], field.at[v, 0], sent.at[4], vec_sem.at[v, inner])
+
+    loads[0].wait()
+    scatter_vec(0)
+    loads[vecs].wait()
+    scatter(own_levels, level, sent.at[5], level_sem)
+    for v in range(1, vecs):
         loads[v].wait()
-        scatter(own.at[v], field.at[v, 0], sent.at[4], vec_sem.at[v])
-        if v == 0:
-            loads[vecs].wait()
-            scatter(own_levels, level, sent.at[5], level_sem)
+
+    @pl.when(jnp.logical_not(mate))
+    def _():
+        for v in range(1, vecs):
+            scatter_vec(v)
 
     loads[vecs + 1].wait()
     values = [own_energies[i] for i in range(energies.shape[0])]
@@ -205,7 +218,7 @@
                 partial_out.at[v, r, z], partial_in.at[v, r, 1 - z],
                 sent.at[1], partial_sem.at[v, r % 2], side + member,
             )
-            for z, side in (((0, behind_base),) if r == ROUNDS - 1 else sides())
+            for z, side in (((1, ahead_base),) if r == ROUNDS - 1 else sides())
         ]
 
     def y_copies(v, r, kind):
@@ -287,7 +300,7 @@
     def partial_faces(v, r):
         for side, (m, inner) in enumerate(((0, 1), (last, last - 1))):
             new = partial(v, 2 * r, m, inner)
-            if r < ROUNDS - 1 or side == 0:
+            if r < ROUNDS - 1 or side == 1:
                 partial_out[v, r, side] = new
             put_edges(v, r, 1, m, new)
         begin(q_copies(v, r))
@@ -301,12 +314,13 @@
         begin(y_copies(v, r, 1))
 
     def arrive(v):
-        drain(field.at[v, 0], vec_sem.at[v])
+        drain(field.at[v, 0, pl.ds(0, 2)], vec_sem.at[v, 0])
         for z, m in ((0, 0), (1, last)):
             corner_out[v, 0, 2 * z] = field[v, 0, m, 0:1]
             corner_out[v, 0, 2 * z + 1] = field[v, 0, m, rows - 1 : rows]
+        begin(z_copies(v, 0))
+        drain(field.at[v, 0, pl.ds(1, GROUP - 2)], vec_sem.at[v, 1])
         begin(corner_copies(v, 0))
-        begin(z_copies(v, 0))
 
         def edges(m, carry):
             edge_out[v, 0, 0, 0, m] = field[v, 0, m, 0:1]
@@ -368,11 +382,11 @@
         for y in range(2):
             for z, m in ((0, 0), (1, last)):
                 edge[y, m] = edge[y, m] - weight * corner_in[v, r, 2 * z + y]
-        came = partial_in.at[v, r, 1] if final else partial_in.at[v, r]
+        came = partial_in.at[v, r, 0] if final else partial_in.at[v, r]
         if final:
-            _, sums = follow(v, k, 0, field[v, k + 1, 1], sums)
+            _, sums = follow(v, k, last, field[v, k + 1, last - 1], sums)
             drain(came, partial_sem.at[v, r % 2])
-            _, sums = follow(v, k, last, field[v, k + 1, last - 1] + 2.0 * outside(1, last), sums)
+            _, sums = follow(v, k, 0, field[v, k + 1, 1] + 2.0 * outside(0, 0), sums)
         else:
             drain(came, partial_sem.at[v, r % 2])
             for side, m, inner in ((0, 0, 1), (1, last, last - 1)):
@@ -390,12 +404,22 @@
             dots[v][0] = sums[4]
 
     arrive(0)
+
+    @pl.when(mate)
+    def _():
+        drain(level.at[others], sent.at[5])
+        for v in range(1, vecs):
+            scatter_vec(v)
+
     drain(level, level_sem)
-    lax.fori_loop(0, GROUP, look_up, 0)
+    look_up(0, 0)
+    look_up(last, 0)
     for v in range(vecs):
         if v:
             arrive(v)
         partial_faces(v, 0)
+        if v == 0:
+            lax.fori_loop(1, last, look_up, 0)
         partial_rest(v, 0)
     for r in range(ROUNDS):
         for v in range(vecs):
@@ -415,13 +439,16 @@
         return carry
 
     lax.fori_loop(1, count, tell, 0, unroll=8)
-    others = pl.ds(0, GROUP - 1)
     drain(plane_in, sent.at[0])
     drain(field.at[:, 0, pl.ds(0, 2 * ROUNDS - 1)], sent.at[1])
     drain(edge_out, sent.at[2])
     drain(corner_out, sent.at[3])
     drain(field.at[:, 0, others], sent.at[4])
-    drain(level.at[others], sent.at[5])
+
+    @pl.when(jnp.logical_not(mate))
+    def _():
+        drain(level.at[others], sent.at[5])
+
     drain(field.at[:, pl.ds(1, RETURNED), others], sent.at[6])
     drain(back, back_sem)
     drain(slots.at[pl.ds(0, count - 1)], sum_sem.at[0])
@@ -492,7 +519,7 @@
             pltpu.VMEM((count, 1, 128), f32),
             pltpu.VMEM((1, 128), f32),
             dma((vecs + 2,)),
-            dma((vecs,)),
+            dma((vecs, 2)),
             dma,
             dma((vecs, 2)),
             dma((vecs, 2)),

time: 45.2 us -> 44.8 us (level)
  no operation moved by 1% of the time
where the time goes in v4:
time: 44.8 us; the launch traced here: 44.7 us
  Pallas kernels  44 us (98%)
  between operations  0.64 us (1%)
    pallas_call x1, Pallas kernels, shards(): pl.pallas_call(functools.partial(kernel, count), out_shape=(jax.ShapeDtyp...  42.9 us
    pallas_call x1, Pallas kernels, shards(): pl.pallas_call(finish, out_shape=(jax.ShapeDtypeStruct(start_vectors.shap...  1.11 us

profile of v4, /device:TPU:0, one launch (start us, length us, event | category | flops | bytes accessed | tf_op | source)
XLA Modules:
  0.0 44.7 jit_solution(9050078950717047251)
XLA Ops:
  0.6 42.9 %shard_map.66 = (f32[2,256,256]{2,1,0:T(8,128)S(1)}, f32[3,2,256,256]{3,2,1,0:T(8,128)S(1)}, f32[4,2,128]{2,1,0:T(2,128)S(1)}) custom-call(f32[16]{0:T(128)} %energies.1, f32[2,1,256,256]{3,2,1,0:T(8,128)} %start.1, s32[1,256,256]{2,1,0:T(8,128)} %levels.1), custom_call_target="tpu_custom_call" | custom-call | tf_op jit(solution)/shard_map/pallas_call | solution.py:496
  43.6 1.1 %shard_map.67 = (f32[2,1,256,256]{3,2,1,0:T(8,128)}, f32[2,8]{1,0:T(2,128)}, f32[2,7]{1,0:T(2,128)}, f32[2,6]{1,0:T(2,128)}) custom-call(f32[2,256,256]{2,1,0:T(8,128)S(1)} %get-tuple-element.7.own, f32[3,2,256,256]{3,2,1,0:T(8,128)S(1)} %get-tuple-element.8.back, f32[4,2,128]{2,1,0:T(2,128)S(1)} %get-tuple-element.9.small), custom_call_target="tpu_custom_call" | custom-call | tf_op jit(solution)/shard_map/pallas_call | solution.py:536

commit v5 on v4

--- a/solution.py
+++ b/solution.py
@@ -221,11 +221,11 @@
             for z, side in (((1, ahead_base),) if r == ROUNDS - 1 else sides())
         ]
 
-    def y_copies(v, r, kind):
+    def y_copies(v, r):
         return [
             remote(
-                edge_out.at[v, r, kind, y], edge_in.at[v, r, kind, 1 - y],
-                sent.at[2], edge_sem.at[v, r % 2, kind], base + place,
+                edge_out.at[v, r, y], edge_in.at[v, r, 1 - y],
+                sent.at[2], edge_sem.at[v, r % 2], base + place,
             )
             for y, place in ((0, above), (1, below))
         ]
@@ -249,8 +249,8 @@
         corner_out[v, r, 2 * z + 1] = value[rows - 1 : rows]
 
     def put_edges(v, r, kind, m, value):
-        edge_out[v, r, kind, 0, m] = value[0:1]
-        edge_out[v, r, kind, 1, m] = value[rows - 1 : rows]
+        edge_out[v, r, 0, kind, m] = value[0:1]
+        edge_out[v, r, 1, kind, m] = value[rows - 1 : rows]
 
     def around(here, top, bottom):
         up, down = pltpu.roll(here, 1, 0), pltpu.roll(here, rows - 1, 0)
@@ -311,7 +311,7 @@
             return carry
 
         lax.fori_loop(1, last, body, 0, unroll=2)
-        begin(y_copies(v, r, 1))
+        begin(y_copies(v, r))
 
     def arrive(v):
         drain(field.at[v, 0, pl.ds(0, 2)], vec_sem.at[v, 0])
@@ -324,11 +324,10 @@
 
         def edges(m, carry):
             edge_out[v, 0, 0, 0, m] = field[v, 0, m, 0:1]
-            edge_out[v, 0, 0, 1, m] = field[v, 0, m, rows - 1 : rows]
+            edge_out[v, 0, 1, 0, m] = field[v, 0, m, rows - 1 : rows]
             return carry
 
         lax.fori_loop(0, GROUP, edges, 0, unroll=True)
-        begin(y_copies(v, 0, 0))
 
     nothing = jnp.zeros((8, lanes), jnp.float32)
     dots = [[None] * (2 * LANCZOS) for v in range(vecs)]
@@ -338,14 +337,14 @@
         final = r == ROUNDS - 1
         weight = 0.5 * scale if k == 0 else scale
 
-        drain(edge_in.at[v, r, 0], edge_sem.at[v, r % 2, 0])
+        drain(edge_in.at[v, r], edge_sem.at[v, r % 2])
 
         def complete(m, carry):
             field[v, k + 1, m, 0:8] = field[v, k + 1, m, 0:8] - jnp.where(
                 sub == 0, weight * edge_in[v, r, 0, 0, m], 0.0
             )
             field[v, k + 1, m, rows - 8 : rows] = field[v, k + 1, m, rows - 8 : rows] - jnp.where(
-                sub == 7, weight * edge_in[v, r, 0, 1, m], 0.0
+                sub == 7, weight * edge_in[v, r, 1, 0, m], 0.0
             )
             return carry
 
@@ -356,11 +355,10 @@
         if r == 0:
             give_back(v, 1)
 
-        drain(edge_in.at[v, r, 1], edge_sem.at[v, r % 2, 1])
         if r in (1, 2):
             give_back(v, r + 1)
         for y in range(2):
-            edge[y] = edge_in[v, r, 1, y] - weight * edge_out[v, r, 0, y]
+            edge[y] = edge_in[v, r, y, 1] - weight * edge_out[v, r, y, 0]
 
         def outside(side, m):
             here = field[v, k, m] + jnp.concatenate(
@@ -394,7 +392,6 @@
                 put_corners(v, r + 1, side, new)
             begin(corner_copies(v, r + 1))
             begin(z_copies(v, r + 1))
-            begin(y_copies(v, r + 1, 0))
             partial_faces(v, r + 1)
             partial_rest(v, r + 1)
         dots[v][2 * k + 1 : 2 * k + 4] = sums[:3]
@@ -523,7 +520,7 @@
             dma,
             dma((vecs, 2)),
             dma((vecs, 2)),
-            dma((vecs, 2, 2)),
+            dma((vecs, 2)),
             dma((vecs, 2)),
             dma,
             dma((2,)),

time: 44.8 us -> 44.7 us (level)
  no operation moved by 1% of the time
where the time goes in v5:
time: 44.7 us; the launch traced here: 44.6 us
  Pallas kernels  43.9 us (98%)
  between operations  0.64 us (1%)
    pallas_call x1, Pallas kernels, shards(): pl.pallas_call(functools.partial(kernel, count), out_shape=(jax.ShapeDtyp...  42.8 us
    pallas_call x1, Pallas kernels, shards(): pl.pallas_call(finish, out_shape=(jax.ShapeDtypeStruct(start_vectors.shap...  1.11 us

profile of v5, /device:TPU:0, one launch (start us, length us, event | category | flops | bytes accessed | tf_op | source)
XLA Modules:
  0.0 44.6 jit_solution(13257727810284683642)
XLA Ops:
  0.6 42.8 %shard_map.66 = (f32[2,256,256]{2,1,0:T(8,128)S(1)}, f32[3,2,256,256]{3,2,1,0:T(8,128)S(1)}, f32[4,2,128]{2,1,0:T(2,128)S(1)}) custom-call(f32[16]{0:T(128)} %energies.1, f32[2,1,256,256]{3,2,1,0:T(8,128)} %start.1, s32[1,256,256]{2,1,0:T(8,128)} %levels.1), custom_call_target="tpu_custom_call" | custom-call | tf_op jit(solution)/shard_map/pallas_call | solution.py:493
  43.4 1.1 %shard_map.67 = (f32[2,1,256,256]{3,2,1,0:T(8,128)}, f32[2,8]{1,0:T(2,128)}, f32[2,7]{1,0:T(2,128)}, f32[2,6]{1,0:T(2,128)}) custom-call(f32[2,256,256]{2,1,0:T(8,128)S(1)} %get-tuple-element.7.own, f32[3,2,256,256]{3,2,1,0:T(8,128)S(1)} %get-tuple-element.8.back, f32[4,2,128]{2,1,0:T(2,128)S(1)} %get-tuple-element.9.small), custom_call_target="tpu_custom_call" | custom-call | tf_op jit(solution)/shard_map/pallas_call | solution.py:533

commit v6 on v5

--- a/solution.py
+++ b/solution.py
@@ -472,16 +472,28 @@
         small[n] = value
 
 
-def finish(own, back, small, cheb, diag, offd, moments):
-    vecs, lanes = own.shape[0], own.shape[2]
+def finish(own, back, small, cheb, diag, offd, moments, mixed, diag_at, offd_at, moments_at, mixed_sem, small_sem):
+    vecs, height, lanes = own.shape
+    copies = []
+    for n, (at, ref) in enumerate(((diag_at, diag), (offd_at, offd), (moments_at, moments))):
+        at[...] = small[n + 1, :, : at.shape[1]]
+        copies.append(pltpu.make_async_copy(at, ref, small_sem.at[n]))
+        copies[-1].start()
+    step = height // 2
+    third = [
+        [jnp.broadcast_to(small[0, v : v + 1, k : k + 1], (1, lanes)) for k in range(RETURNED + 1)] for v in range(vecs)
+    ]
     for v in range(vecs):
-        third = [jnp.broadcast_to(small[0, v : v + 1, k : k + 1], (1, lanes)) for k in range(RETURNED + 1)]
-        value = third[0] * own[v]
-        for k in range(RETURNED):
-            value = value + third[k + 1] * back[k, v]
-        cheb[v, 0] = value
-    for n, ref in enumerate((diag, offd, moments)):
-        ref[...] = small[n + 1, :, : ref.shape[1]]
+        for i in range(2):
+            part = pl.ds(i * step, step)
+            value = third[v][0] * own[v, part]
+            for k in range(RETURNED):
+                value = value + third[v][k + 1] * back[k, v, part]
+            mixed[v, part] = value
+            pltpu.make_async_copy(mixed.at[v, part], cheb.at[v, 0, part], mixed_sem).start()
+    for copy in copies:
+        copy.wait()
+    pltpu.make_async_copy(mixed, mixed, mixed_sem).wait()
 
 
 def shards(count, start_vectors, levels, energies):
@@ -539,7 +551,15 @@
             jax.ShapeDtypeStruct((vecs, 6), f32),
         ),
         in_specs=[vmem] * 3,
-        out_specs=(vmem,) * 4,
+        out_specs=(pl.BlockSpec(memory_space=pltpu.HBM),) * 4,
+        scratch_shapes=[
+            pltpu.VMEM((vecs, height, lanes), f32),
+            pltpu.VMEM((vecs, LANCZOS), f32),
+            pltpu.VMEM((vecs, LANCZOS - 1), f32),
+            pltpu.VMEM((vecs, 6), f32),
+            dma,
+            dma((3,)),
+        ],
         compiler_params=pltpu.CompilerParams(vmem_limit_bytes=VMEM_BYTES),
     )(*kept)
 

time: 44.7 us -> 44.6 us (level)
  no operation moved by 1% of the time
where the time goes in v6:
time: 44.6 us; the launch traced here: 44.4 us
  Pallas kernels  43.8 us (98%)
  between operations  0.64 us (1%)
    pallas_call x1, Pallas kernels, shards(): pl.pallas_call(functools.partial(kernel, count), out_shape=(jax.ShapeDtyp...  42.8 us
    pallas_call x1, Pallas kernels, shards(): pl.pallas_call(finish, out_shape=(jax.ShapeDtypeStruct(start_vectors.shap...  0.97 us

profile of v6, /device:TPU:0, one launch (start us, length us, event | category | flops | bytes accessed | tf_op | source)
XLA Modules:
  0.0 44.4 jit_solution(13584173163874661991)
XLA Ops:
  0.6 42.8 %shard_map.66 = (f32[2,256,256]{2,1,0:T(8,128)S(1)}, f32[3,2,256,256]{3,2,1,0:T(8,128)S(1)}, f32[4,2,128]{2,1,0:T(2,128)S(1)}) custom-call(f32[16]{0:T(128)} %energies.1, f32[2,1,256,256]{3,2,1,0:T(8,128)} %start.1, s32[1,256,256]{2,1,0:T(8,128)} %levels.1), custom_call_target="tpu_custom_call" | custom-call | tf_op jit(solution)/shard_map/pallas_call | solution.py:505
  43.4 1.0 %shard_map.67 = (f32[2,1,256,256]{3,2,1,0:T(8,128)}, f32[2,8]{1,0:T(2,128)}, f32[2,7]{1,0:T(2,128)}, f32[2,6]{1,0:T(2,128)}) custom-call(f32[2,256,256]{2,1,0:T(8,128)S(1)} %get-tuple-element.7.own, f32[3,2,256,256]{3,2,1,0:T(8,128)S(1)} %get-tuple-element.8.back, f32[4,2,128]{2,1,0:T(2,128)S(1)} %get-tuple-element.9.small), custom_call_target="tpu_custom_call" | custom-call | tf_op jit(solution)/shard_map/pallas_call | solution.py:545
